TPU v7x, 8 devices: a whole 2x2x1 slice. The times are simulated.
8 devices in a mesh: dp: 2 (over z, y), tp: 4 (over x, core).
Axes of the slice: x: 2, y: 2, z: 1, core: 2. Of those that a mesh axis runs over, the one named last changes fastest.
Arguments:
- x_in: bfloat16 [2048, 3072], P(('dp', 'tp')), parts along dimension 0
- grad_y: bfloat16 [2048, 3072], P(('dp', 'tp')), parts along dimension 0
- norm_gain: float32 [2, 3072], replicated
- w_qkv: bfloat16 [2, 3072, 5120], P(None, None, 'tp')
- w_out: bfloat16 [2, 3072, 3072], P(None, 'tp')
- w_gate: bfloat16 [2, 3072, 8192], P(None, None, 'tp')
- w_up: bfloat16 [2, 3072, 8192], P(None, None, 'tp')
- w_down: bfloat16 [2, 8192, 3072], P(None, 'tp')
Outputs:
- output 1: bfloat16 [2048, 3072], P(('dp', 'tp')), parts along dimension 0
- output 2: float32 [4, 3072], P('dp'), parts along dimension 0
- output 3: bfloat16 [4, 3072, 5120], P('dp', None, 'tp'), parts along dimension 0
- output 4: bfloat16 [4, 3072, 3072], P('dp', 'tp'), parts along dimension 0
- output 5: bfloat16 [4, 3072, 8192], P('dp', None, 'tp'), parts along dimension 0
- output 6: bfloat16 [4, 3072, 8192], P('dp', None, 'tp'), parts along dimension 0
- output 7: bfloat16 [4, 8192, 3072], P('dp', 'tp'), parts along dimension 0
There are 2 independent parts. A program takes and returns all parts, laid end to end along the dimension named above; an argument that names none is the same for every part.
All inputs are finite; a program needn't handle non-finite values.
Results may differ from a plain program's by a relative error of at most 0.015981.
Values are sent between devices in bfloat16 or wider.
A program may use at most 1 GiB of HBM per device.

v0:
```python
import jax
import jax.numpy as jnp
from jax import lax
from jax.experimental import pallas as pl
from jax.experimental.pallas import tpu as pltpu
from jax.sharding import PartitionSpec as P


HEAD_DIM = 128
NORM_EPS = 1e-5
ROPE_BASE = 10000.0
BF16 = jnp.bfloat16
F32 = jnp.float32
GROUP = 3
SCALE = HEAD_DIM ** -0.5
CORE_PAIRS = [(0, 1), (1, 0), (2, 3), (3, 2)]
CHIP_PAIRS = [(0, 2), (2, 0), (1, 3), (3, 1)]
VMEM_LIMIT = 40 << 20
MM_VMEM = 28 << 20
WG_VMEM = 36 << 20


def core_swap(values):
    return lax.ppermute(values, 'tp', CORE_PAIRS)


def chip_swap(values):
    return lax.ppermute(values, 'tp', CHIP_PAIRS)


def barrier(*values):
    return lax.optimization_barrier(values)


def rope_tables(seq_len):
    half_dim = HEAD_DIM // 2
    freqs = ROPE_BASE ** (-2.0 * jnp.arange(half_dim, dtype=F32) / HEAD_DIM)
    angles = jnp.arange(seq_len, dtype=F32)[:, None] * freqs[None, :]
    cos_tab, sin_tab = jnp.cos(angles), jnp.sin(angles)
    return jnp.concatenate([cos_tab, cos_tab], axis=1), jnp.concatenate([-sin_tab, sin_tab], axis=1)


def rms_scale(x_f32, gain_row):
    inv_rms = lax.rsqrt(jnp.mean(x_f32 * x_f32, axis=-1, keepdims=True) + NORM_EPS)
    return x_f32 * inv_rms * gain_row


def gated(gate_f32, up_f32):
    return jax.nn.silu(gate_f32) * up_f32


def dot(lhs, rhs):
    return jnp.dot(lhs, rhs, preferred_element_type=F32)


def dot_t(lhs, rhs):
    return lax.dot_general(lhs, rhs, (((1,), (1,)), ((), ())), preferred_element_type=F32)


def dot_lt(lhs, rhs):
    return lax.dot_general(lhs, rhs, (((0,), (0,)), ((), ())), preferred_element_type=F32)


def attn_fwd_kernel(base_ref, qn_ref, qf_ref, cos_ref, sin_ref, rq_ref, on_ref, of_ref, lse_ref, o_scr):
    rows = qn_ref.shape[0] // 2
    kcol, vcol = GROUP * HEAD_DIM, (GROUP + 1) * HEAD_DIM
    for k in range(4):
        src = qn_ref if k < 2 else qf_ref
        local = slice((k % 2) * rows, (k % 2 + 1) * rows)
        where = pl.ds(pl.multiple_of(base_ref[k] * rows, rows), rows)
        cos_tab, sin_tab = cos_ref[where, :], sin_ref[where, :]
        for h in range(GROUP + 1):
            cols = slice(h * HEAD_DIM, (h + 1) * HEAD_DIM)
            vals = src[local, cols].astype(F32)
            rq_ref[where, cols] = (vals * cos_tab + pltpu.roll(vals, HEAD_DIM // 2, 1) * sin_tab).astype(BF16)
        rq_ref[where, vcol:] = src[local, vcol:]
    causal = lax.broadcasted_iota(jnp.int32, (rows, rows), 0) >= lax.broadcasted_iota(jnp.int32, (rows, rows), 1)
    for i in range(4):
        width = (i + 1) * rows
        keys, vals = rq_ref[0:width, kcol:vcol], rq_ref[0:width, vcol:]
        for h in range(GROUP):
            query = rq_ref[i * rows:width, h * HEAD_DIM:(h + 1) * HEAD_DIM]
            scores = dot_t(query, keys) * SCALE
            diag = jnp.where(causal, scores[:, i * rows:], -1e30)
            scores = diag if i == 0 else jnp.concatenate([scores[:, :i * rows], diag], axis=1)
            row_max = jnp.max(scores, axis=1, keepdims=True)
            weights = jnp.exp(scores - row_max)
            total = jnp.sum(weights, axis=1, keepdims=True)
            prob = (weights * (1.0 / total)).astype(BF16)
            o_scr[i * rows:width, h * HEAD_DIM:(h + 1) * HEAD_DIM] = dot(prob, vals).astype(BF16)
            lse = jnp.broadcast_to(row_max + jnp.log(total), (rows, HEAD_DIM))
            lse_ref[0, h:h + 1, i * rows:width] = jnp.transpose(lse)[0:1, :]
    for k in range(4):
        dst = on_ref if k < 2 else of_ref
        dst[(k % 2) * rows:(k % 2 + 1) * rows, :] = o_scr[pl.ds(pl.multiple_of(base_ref[k] * rows, rows), rows), :]


def attn_fwd(base, qkv_n, qkv_f, cos_tab, sin_tab):
    half, width = cos_tab.shape[0] // 2, qkv_n.shape[1]
    cols = (GROUP + 2) * HEAD_DIM
    groups = width // cols
    seq_len = 2 * half
    smem = pl.BlockSpec(memory_space=pltpu.SMEM)
    tab = pl.BlockSpec((seq_len, HEAD_DIM), lambda j: (0, 0))
    half_in = pl.BlockSpec((half, cols), lambda j: (0, j))
    half_out = pl.BlockSpec((half, GROUP * HEAD_DIM), lambda j: (0, j))
    return pl.pallas_call(
        attn_fwd_kernel, grid=(groups,), name='attn_fwd',
        in_specs=[smem, half_in, half_in, tab, tab],
        out_specs=[pl.BlockSpec((seq_len, cols), lambda j: (0, j)), half_out, half_out, pl.BlockSpec((1, 8, seq_len), lambda j: (j, 0, 0))],
        out_shape=[out_struct((seq_len, width), BF16, True)] + [jax.ShapeDtypeStruct((half, groups * GROUP * HEAD_DIM), BF16)] * 2 + [jax.ShapeDtypeStruct((groups, 8, seq_len), F32)],
        scratch_shapes=[pltpu.VMEM((seq_len, GROUP * HEAD_DIM), BF16)],
        cost_estimate=pl.CostEstimate(flops=8 * 10 ** 9, bytes_accessed=8 * 10 ** 6, transcendentals=4 * 10 ** 6),
        compiler_params=pltpu.CompilerParams(vmem_limit_bytes=VMEM_LIMIT),
    )(base, qkv_n, qkv_f, cos_tab, sin_tab)


def attn_bwd_kernel(base_ref, rq_ref, lse_ref, dn_ref, df_ref, cos_ref, sin_ref, gn_ref, gf_ref, do_scr, dq_scr, dk_scr, dv_scr):
    rows = dn_ref.shape[0] // 2
    kcol, vcol = GROUP * HEAD_DIM, (GROUP + 1) * HEAD_DIM
    for k in range(4):
        src = dn_ref if k < 2 else df_ref
        do_scr[pl.ds(pl.multiple_of(base_ref[k] * rows, rows), rows), :] = src[(k % 2) * rows:(k % 2 + 1) * rows, :]
    dk_scr[...] = jnp.zeros_like(dk_scr)
    dv_scr[...] = jnp.zeros_like(dv_scr)
    causal = lax.broadcasted_iota(jnp.int32, (rows, rows), 1) >= lax.broadcasted_iota(jnp.int32, (rows, rows), 0)
    for i in range(4):
        width = (i + 1) * rows
        keys, vals = rq_ref[0:width, kcol:vcol], rq_ref[0:width, vcol:]
        for h in range(GROUP):
            cols = slice(h * HEAD_DIM, (h + 1) * HEAD_DIM)
            query, d_o = rq_ref[i * rows:width, cols], do_scr[i * rows:width, cols]
            scores = dot_t(keys, query) * SCALE
            diag = jnp.where(causal, scores[i * rows:, :], -1e30)
            scores = diag if i == 0 else jnp.concatenate([scores[:i * rows, :], diag], axis=0)
            prob = jnp.exp(scores - lse_ref[0, h:h + 1, i * rows:width])
            d_prob = dot_t(vals, d_o).astype(BF16).astype(F32)
            delta = jnp.sum(prob * d_prob, axis=0, keepdims=True)
            d_scores = (prob * (d_prob - delta) * SCALE).astype(BF16)
            dv_scr[0:width, :] += dot(prob.astype(BF16), d_o)
            dk_scr[0:width, :] += dot(d_scores, query)
            dq_scr[i * rows:width, cols] = dot_lt(d_scores, keys).astype(BF16)
    for k in range(4):
        dst = gn_ref if k < 2 else gf_ref
        local = slice((k % 2) * rows, (k % 2 + 1) * rows)
        where = pl.ds(pl.multiple_of(base_ref[k] * rows, rows), rows)
        cos_tab, sin_tab = cos_ref[where, :], sin_ref[where, :]
        for h in range(GROUP + 1):
            cols = slice(h * HEAD_DIM, (h + 1) * HEAD_DIM)
            vals = dq_scr[where, cols].astype(F32) if h < GROUP else dk_scr[where, :].astype(BF16).astype(F32)
            dst[local, cols] = (vals * cos_tab - pltpu.roll(vals, HEAD_DIM // 2, 1) * sin_tab).astype(BF16)
        dst[local, vcol:] = dv_scr[where, :].astype(BF16)


def attn_bwd(base, rot_qkv, lse, d_halves, cos_tab, sin_tab):
    seq_len, width = rot_qkv.shape
    half = seq_len // 2
    cols = (GROUP + 2) * HEAD_DIM
    groups = width // cols
    smem = pl.BlockSpec(memory_space=pltpu.SMEM)
    tab = pl.BlockSpec((seq_len, HEAD_DIM), lambda j: (0, 0))
    halves_in = [pl.BlockSpec((half, GROUP * HEAD_DIM), lambda j, r=r: (r, j)) for _, r in d_halves]
    half_out = pl.BlockSpec((half, cols), lambda j: (0, j))
    return pl.pallas_call(
        attn_bwd_kernel, grid=(groups,), name='attn_bwd',
        in_specs=[smem, pl.BlockSpec((seq_len, cols), lambda j: (0, j)), pl.BlockSpec((1, 8, seq_len), lambda j: (j, 0, 0)), *halves_in, tab, tab],
        out_specs=[half_out, half_out],
        out_shape=[jax.ShapeDtypeStruct((half, width), BF16)] * 2,
        scratch_shapes=[pltpu.VMEM((seq_len, GROUP * HEAD_DIM), BF16)] * 2 + [pltpu.VMEM((seq_len, HEAD_DIM), F32)] * 2,
        cost_estimate=pl.CostEstimate(flops=20 * 10 ** 9, bytes_accessed=8 * 10 ** 6, transcendentals=4 * 10 ** 6),
        compiler_params=pltpu.CompilerParams(vmem_limit_bytes=VMEM_LIMIT),
    )(base, rot_qkv, lse, d_halves[0][0], d_halves[1][0], cos_tab, sin_tab)


def wgrad_kernel(an_ref, af_ref, bn_ref, bf_ref, *rest):
    out_ref = rest[-1]
    out_ref[0] = (dot_lt(an_ref[...], bn_ref[...]) + dot_lt(af_ref[...], bf_ref[...])).astype(BF16)


def wgrad(half, lhs, rhs, layer_idx, n_layers, stacked, block_rows):
    m_dim, n_dim = lhs[0][0].shape[1], rhs[0][0].shape[1]
    in_specs = [pl.BlockSpec((half, block_rows), lambda m, r=r: (r, m)) for _, r in lhs]
    in_specs += [pl.BlockSpec((half, n_dim), lambda m, r=r: (r, 0)) for _, r in rhs]
    args = [arr for arr, _ in lhs + rhs]
    aliases = {}
    if stacked is not None:
        in_specs.append(pl.BlockSpec(memory_space=pl.ANY))
        args.append(stacked)
        aliases = {4: 0}
    return pl.pallas_call(
        wgrad_kernel, grid=(m_dim // block_rows,), in_specs=in_specs,
        out_specs=pl.BlockSpec((1, block_rows, n_dim), lambda m: (layer_idx, m, 0)),
        out_shape=jax.ShapeDtypeStruct((n_layers, m_dim, n_dim), BF16),
        input_output_aliases=aliases,
        cost_estimate=pl.CostEstimate(flops=4 * half * m_dim * n_dim, bytes_accessed=2 * (m_dim * n_dim + 2 * half * (m_dim + n_dim)), transcendentals=0),
        compiler_params=pltpu.CompilerParams(vmem_limit_bytes=WG_VMEM),
    )(*args)


def out_struct(shape, dtype, in_hbm=False):
    return pltpu.HBM(shape, dtype) if in_hbm else jax.ShapeDtypeStruct(shape, dtype)


def fused_mm(rows, xs, ws, trans, layer, block, extras, epilogue, outs, first=0, steps=None):
    steps = (ws[0].shape[1] if trans else ws[0].shape[2]) // block if steps is None else steps
    n_dim = steps * block
    n_x, n_e = len(xs), len(extras)

    def kernel(*refs):
        accs = [(dot_t if trans else dot)(refs[i][...], refs[n_x + i][0]) for i in range(n_x)]
        results = epilogue(accs, [ref[...] for ref in refs[2 * n_x:2 * n_x + n_e]])
        for ref, val in zip(refs[2 * n_x + n_e:], results):
            ref[...] = val.astype(ref.dtype)

    in_specs = [pl.BlockSpec((rows, x.shape[1]), lambda n, r=r: (r, 0)) for x, r in xs]
    if trans:
        in_specs += [pl.BlockSpec((1, block, w.shape[2]), lambda n: (layer, n + first, 0)) for w in ws]
    else:
        in_specs += [pl.BlockSpec((1, w.shape[1], block), lambda n: (layer, 0, n + first)) for w in ws]
    in_specs += [pl.BlockSpec((rows, block), lambda n, r=r: (r, n)) for _, r in extras]
    depth = sum(x.shape[1] for x, _ in xs)
    return list(pl.pallas_call(
        kernel, grid=(steps,), in_specs=in_specs,
        out_specs=[pl.BlockSpec((r, block), lambda n: (0, n)) for r, *_ in outs],
        out_shape=[out_struct((r, n_dim), *rest) for r, *rest in outs],
        cost_estimate=pl.CostEstimate(flops=2 * rows * depth * n_dim, bytes_accessed=2 * depth * (rows + n_dim) + 4 * rows * n_dim, transcendentals=0),
        compiler_params=pltpu.CompilerParams(vmem_limit_bytes=MM_VMEM),
    )(*[x for x, _ in xs], *ws, *[e for e, _ in extras]))


def gate_up_epilogue(accs, extras):
    gate, up = accs[0].astype(BF16), accs[1].astype(BF16)
    return gate, up, gated(gate.astype(F32), up.astype(F32))


def gate_up_back_epilogue(accs, extras):
    gate, up = accs[0].astype(BF16).astype(F32), accs[1].astype(BF16).astype(F32)
    hidden, pull = jax.vjp(gated, gate, up)
    return (hidden,) + pull(extras[0].astype(F32))


def split_sum_epilogue(accs, extras):
    total = sum(accs[1:], accs[0])
    rows = total.shape[0] // 2
    return total[:rows], total[rows:]


def mlp_back_epilogue(accs, extras):
    d_hid = accs[0].astype(BF16).astype(F32)
    gate, up = extras[0].astype(F32), extras[1].astype(F32)
    hidden, pull = jax.vjp(gated, gate, up)
    return (hidden,) + pull(d_hid)


def solution(mesh):
    row_spec = P(('dp', 'tp'), None)
    col_spec = P(None, None, 'tp')
    inner_spec = P(None, 'tp', None)

    def device_program(x_loc, dy_loc, norm_gain, w_qkv, w_out, w_gate, w_up, w_down):
        n_layers = w_qkv.shape[0]
        rows = x_loc.shape[0]
        half = 2 * rows
        rank = lax.axis_index('tp')
        base = jnp.bitwise_xor(jnp.arange(4, dtype=jnp.int32), rank.astype(jnp.int32))
        cos_tab, sin_tab = rope_tables(4 * rows)
        saved = []
        x_cur = x_loc

        def project(layer, u_half, d_hid):
            qkv = dot(u_half, w_qkv[layer]).astype(BF16)
            extras = [] if d_hid is None else [(d_hid, 0)]
            epilogue = gate_up_epilogue if d_hid is None else gate_up_back_epilogue
            return [qkv] + fused_mm(half, [(u_half, 0)] * 2, [w_gate, w_up], False, layer, 256, extras, epilogue, [(half, BF16, True)] * 2 + [(half, BF16, d_hid is not None)])

        def mlp_back(layer, n_rows, dy_half, gate_half, up_half):
            return fused_mm(n_rows, [(dy_half, 0)], [w_down], True, layer, 256, [(gate_half, 0), (up_half, 0)], mlp_back_epilogue, [(n_rows, BF16)] * 3)

        def wgrads(which, layer, u_halves, d_qkv, d_gate, d_up, o_halves, hidden, dy_halves, stacks):
            lhs = {0: u_halves, 1: o_halves, 2: u_halves, 3: u_halves, 4: hidden}[which]
            rhs = {0: d_qkv, 1: dy_halves, 2: d_gate, 3: d_up, 4: dy_halves}[which]
            stacks[which] = wgrad(half, list(lhs), list(rhs), layer, n_layers, stacks[which], 256 if which == 1 else 512)

        d_hid1 = dy_far = None
        for layer in range(n_layers):
            last = layer == n_layers - 1
            x_f32 = x_cur.astype(F32)
            u_loc = rms_scale(x_f32, norm_gain[layer]).astype(BF16)
            other = chip_swap(u_loc)
            u_near = jnp.concatenate([u_loc, core_swap(u_loc)], axis=0)
            near = project(layer, u_near, d_hid1[0] if last else None)
            if layer == 0:
                dy_core = core_swap(dy_loc)
                dy_near = jnp.concatenate([dy_loc, dy_core], axis=0)
                d_attn1_n = dot_t(dy_near, w_out[n_layers - 1]).astype(BF16)
                near[0], near[1], d_attn1_n, other = barrier(near[0], near[1], d_attn1_n, other)
            else:
                near[0], near[1], other = barrier(near[0], near[1], other)
            u_far = jnp.concatenate([other, core_swap(other)], axis=0)
            if layer == 0:
                dy_start, u_far = barrier(dy_loc, u_far)
                dy_other = chip_swap(dy_start)
            far = project(layer, u_far, d_hid1[1] if last else None)
            rot_qkv, o_n, o_f, lse = attn_fwd(base, near[0], far[0], cos_tab, sin_tab)
            saved.append({'x': x_cur, 'u': u_loc, 'rot': rot_qkv, 'o': ((o_n, 0), (o_f, 0)), 'lse': lse, 'gate': (near[1], far[1]), 'up': (near[2], far[2])})
            if last:
                break
            split_outs = [(rows, F32)] * 2
            n_cols = x_f32.shape[1] // 512 // 2

            def out_far(o_half, first):
                return fused_mm(half, [(o_half, 0), (far[3], 0)], [w_out, w_down], False, layer, 512, [], split_sum_epilogue, split_outs, first, n_cols)

            keep_a, send_a = out_far(o_f, 0)
            recv_a = core_swap(send_a)
            o_f, send_a = barrier(o_f, send_a)
            keep_b, send_b = out_far(o_f, n_cols)
            recv_b = core_swap(send_b)
            recv_a, keep_b = barrier(recv_a, keep_b)
            sum_a = keep_a + recv_a
            far_a = chip_swap(sum_a)
            o_n, near[3], sum_a = barrier(o_n, near[3], sum_a)
            near_keep, near_send = fused_mm(half, [(o_n, 0), (near[3], 0)], [w_out, w_down], False, layer, 512, [], split_sum_epilogue, split_outs)
            near_recv = core_swap(near_send)
            recv_b, near_keep = barrier(recv_b, near_keep)
            sum_b = keep_b + recv_b
            far_b = chip_swap(sum_b)
            if layer == 0:
                dy_near, dy_other, sum_b = barrier(dy_near, dy_other, sum_b)
                dy_far = jnp.concatenate([dy_other, core_swap(dy_other)], axis=0)
                d_attn1_f = dot_t(dy_far, w_out[n_layers - 1]).astype(BF16)
                d_hid1 = [dot_t(dy_half, w_down[n_layers - 1]).astype(BF16) for dy_half in (dy_near, dy_far)]
            x_sum = x_f32 + (near_keep + near_recv)
            x_sum, d_hid1[0], d_hid1[1], d_attn1_f, far_a, far_b = barrier(x_sum, d_hid1[0], d_hid1[1], d_attn1_f, far_a, far_b)
            x_cur = (x_sum + jnp.concatenate([far_a, far_b], axis=1)).astype(BF16)
        u_halves = ((u_near, 0), (u_far, 0))
        grad_cur = dy_loc
        stacks = [None] * 5
        gain_grads = [None] * n_layers
        for layer in reversed(range(n_layers)):
            kept = saved[layer]
            (gate_n, gate_f), (up_n, up_f) = kept['gate'], kept['up']
            if layer == n_layers - 1:
                dy_halves = ((dy_near, 0), (dy_far, 0))
                d_attn = ((d_attn1_n, 0), (d_attn1_f, 0))
            else:
                dy_near = jnp.concatenate([grad_cur, core_swap(grad_cur)], axis=0)
                dy_other = chip_swap(grad_cur)
                d_attn_near = dot_t(dy_near, w_out[layer]).astype(BF16)
            if layer == n_layers - 1:
                back_n, back_f = near[1:], far[1:]
            else:
                back_n = mlp_back(layer, half, dy_near, gate_n, up_n)
                stacks[4], back_n[0], dy_other = barrier(stacks[4], back_n[0], dy_other)
                dy_far = jnp.concatenate([dy_other, core_swap(dy_other)], axis=0)
                dy_halves = ((dy_near, 0), (dy_far, 0))
                d_attn_far = dot_t(dy_far, w_out[layer]).astype(BF16)
                d_attn = ((d_attn_near, 0), (d_attn_far, 0))
                back_f = mlp_back(layer, half, dy_far, gate_f, up_f)
                u_start, stacks[0], stacks[2], stacks[3], dy_other = barrier(kept['u'], stacks[0], stacks[2], stacks[3], dy_other)
                u_other = chip_swap(u_start)
                u_near = jnp.concatenate([u_start, core_swap(u_start)], axis=0)
                u_far = jnp.concatenate([u_other, core_swap(u_other)], axis=0)
                u_halves = ((u_near, 0), (u_far, 0))
            hidden, d_gate, d_up = [((back_n[idx], 0), (back_f[idx], 0)) for idx in range(3)]
            qkv_n, qkv_f = attn_bwd(base, kept['rot'], kept['lse'], d_attn, cos_tab, sin_tab)
            d_qkv = ((qkv_n, 0), (qkv_f, 0))
            w_args = (layer, u_halves, d_qkv, d_gate, d_up, kept['o'], hidden, dy_halves, stacks)

            def dgrad(side):
                return fused_mm(half, [d_qkv[side], d_gate[side], d_up[side]], [w_qkv, w_gate, w_up], True, layer, 512, [], split_sum_epilogue, [(rows, F32)] * 2)

            far_keep, far_send = dgrad(1)
            far_recv = core_swap(far_send)
            wgrads(1, *w_args)
            stacks[1], far_recv = barrier(stacks[1], far_recv)
            far_sum = far_keep + far_recv
            from_far = chip_swap(far_sum)
            qkv_n, far_sum = barrier(qkv_n, far_sum)
            d_qkv = ((qkv_n, 0), (qkv_f, 0))
            near_keep, near_send = dgrad(0)
            near_recv = core_swap(near_send)
            w_args = (layer, u_halves, d_qkv, d_gate, d_up, kept['o'], hidden, dy_halves, stacks)
            wgrads(0, *w_args)
            wgrads(2, *w_args)
            wgrads(3, *w_args)
            if layer == 0:
                wgrads(4, *w_args)
                stacks[4], from_far = barrier(stacks[4], from_far)
            stacks[0], stacks[2], stacks[3], from_far = barrier(stacks[0], stacks[2], stacks[3], from_far)
            d_normed = (near_keep + near_recv + from_far).astype(BF16)
            norm_pull = jax.vjp(rms_scale, kept['x'].astype(F32), norm_gain[layer])[1]
            d_x_norm, gain_grads[layer] = norm_pull(d_normed.astype(F32))
            grad_cur = (grad_cur.astype(F32) + d_x_norm).astype(BF16)
            if layer != 0:
                dy_halves = tuple(dy_halves)
                hid_n, hid_f, grad_tie = barrier(back_n[0], back_f[0], grad_cur)
                grad_cur = grad_tie
                w_args = (layer, u_halves, d_qkv, d_gate, d_up, kept['o'], ((hid_n, 0), (hid_f, 0)), dy_halves, stacks)
                wgrads(4, *w_args)
        gain = jnp.stack(gain_grads)
        gain = gain + core_swap(gain)
        gain = gain + chip_swap(gain)
        return (grad_cur, gain, stacks[0], stacks[1], stacks[2], stacks[3], stacks[4])

    return jax.shard_map(device_program, mesh=mesh, in_specs=(row_spec, row_spec, P(None, None), col_spec, inner_spec, col_spec, col_spec, inner_spec), out_specs=(row_spec, P('dp', None), P('dp', None, 'tp'), P('dp', 'tp', None), P('dp', None, 'tp'), P('dp', None, 'tp'), P('dp', 'tp', None)), check_vma=False)
```

profile of v0, /device:TPU:0, one launch (start us, length us, event | category | flops | bytes accessed | tf_op | source)
XLA Modules:
  0.0 632.2 jit_solution(8047180009705406411)
XLA Ops:
  2.9 1.8 fusion.44
  4.8 2.1 fusion.34
  6.9 2.9 collective-permute-start.2
  10.1 3.5 fusion.65.dn_ref
  13.7 3.4 copy-done.45
  17.0 5.3 fusion.53.qn_ref
  22.5 18.8 %shard_map.135 = (bf16[512,2048]{1,0:T(8,128)(2,1)}, bf16[512,2048]{1,0:T(8,128)(2,1)}, bf16[512,2048]{1,0:T(8,128)(2,1)S(1)}) custom-call(bf16[512,3072]{1,0:T(8,128)(2,1)S(1)} %pad_maximum_fusion.refs_0_.refs_1_, bf16[512,3072]{1,0:T(8,128)(2,1)S(1)} %pad_maximum_fusion.refs_0_.refs_1_, bf16[2,3072,2048]{2,1,0:T(8,128)(2,1)} %refs_4_.7, ...), custom_call_target="tpu_custom_call" | custom-call | flops 12884901888 | bytes 35651584 | tf_op jit(solution)/shard_map/pallas_call | solution.py:222
  41.3 3.2 collective-permute-done.2
  44.6 2.0 fusion.79
  48.3 2.1 pad_maximum_fusion.1.refs_0_.refs_1_
  50.4 6.7 %fusion.56.qf_ref = bf16[512,1280]{1,0:T(8,128)(2,1)S(1)} fusion(bf16[512,3072]{1,0:T(8,128)(2,1)S(1)} %pad_maximum_fusion.1.refs_0_.refs_1_, bf16[2,3072,1280]{2,1,0:T(8,128)(2,1)} %refs_3_.21), kind=kOutput, calls=%fused_computation.71 | convolution fusion | flops 4027187200 | bytes 12320768 | tf_op jit(solution)/shard_map/dot_general | solution.py:53
  57.1 18.4 %shard_map.136 = (bf16[512,2048]{1,0:T(8,128)(2,1)}, bf16[512,2048]{1,0:T(8,128)(2,1)}, bf16[512,2048]{1,0:T(8,128)(2,1)S(1)}) custom-call(bf16[512,3072]{1,0:T(8,128)(2,1)S(1)} %pad_maximum_fusion.1.refs_0_.refs_1_, bf16[512,3072]{1,0:T(8,128)(2,1)S(1)} %pad_maximum_fusion.1.refs_0_.refs_1_, bf16[2,3072,2048]{2,1,0:T(8,128)(2,1)} %refs_4_.7, ...), custom_call_target="tpu_custom_call" | custom-call | flops 12884901888 | bytes 35651584 | tf_op jit(solution)/shard_map/pallas_call | solution.py:222
  75.5 14.1 %attn_fwd.2 = (bf16[1024,1280]{1,0:T(8,128)(2,1)}, bf16[512,768]{1,0:T(8,128)(2,1)S(1)}, bf16[512,768]{1,0:T(8,128)(2,1)S(1)}, f32[2,8,1024]{2,1,0:T(8,128)S(1)}) custom-call(s32[4]{0:T(128)S(1)} %iota_xor_fusion.base_ref, bf16[512,1280]{1,0:T(8,128)(2,1)S(1)} %copy-done.42, bf16[512,1280]{1,0:T(8,128)(2,1)S(1)} %fusion.56.qf_ref, ...), custom_call_target="tpu_custom_call" | custom-call | flops 8000000000 | bytes 8000000 | tf_op jit(solution)/shard_map/attn_fwd/pallas_call | solution.py:107
  89.7 7.3 %shard_map.137 = (f32[256,1536]{1,0:T(8,128)S(1)}, f32[256,1536]{1,0:T(8,128)S(1)}) custom-call(bf16[512,768]{1,0:T(8,128)(2,1)S(1)} %get-tuple-element.108.refs_0_.af_ref, bf16[512,2048]{1,0:T(8,128)(2,1)S(1)} %get-tuple-element.106.refs_1_, bf16[2,768,3072]{2,1,0:T(8,128)(2,1)S(1)} %bitcast.58, bf16[2,2048,3072]{2,1,0:T(8,128)(2,1)} %refs_1_.3), custom_call_target="tpu_custom_call" | custom-call | flops 4429185024 | bytes 14680064 | tf_op jit(solution)/shard_map/pallas_call | solution.py:222
  97.2 7.0 %shard_map.138 = (f32[256,1536]{1,0:T(8,128)S(1)}, f32[256,1536]{1,0:T(8,128)S(1)}) custom-call(bf16[512,768]{1,0:T(8,128)(2,1)S(1)} %get-tuple-element.108.refs_0_.af_ref, bf16[512,2048]{1,0:T(8,128)(2,1)S(1)} %get-tuple-element.106.refs_1_, bf16[2,768,3072]{2,1,0:T(8,128)(2,1)S(1)} %bitcast.58, bf16[2,2048,3072]{2,1,0:T(8,128)(2,1)} %refs_1_.3), custom_call_target="tpu_custom_call" | custom-call | flops 4429185024 | bytes 14680064 | tf_op jit(solution)/shard_map/pallas_call | solution.py:222
  104.5 1.7 collective-permute-start.7
  108.0 12.9 %shard_map.139 = (f32[256,3072]{1,0:T(8,128)S(1)}, f32[256,3072]{1,0:T(8,128)}) custom-call(bf16[512,768]{1,0:T(8,128)(2,1)S(1)} %get-tuple-element.115.refs_0_.an_ref, bf16[512,2048]{1,0:T(8,128)(2,1)S(1)} %get-tuple-element.116.refs_1_, bf16[2,768,3072]{2,1,0:T(8,128)(2,1)S(1)} %bitcast.58, bf16[2,2048,3072]{2,1,0:T(8,128)(2,1)} %refs_1_.3), custom_call_target="tpu_custom_call" | custom-call | flops 8858370048 | bytes 26476544 | tf_op jit(solution)/shard_map/pallas_call | solution.py:222
  122.2 1.7 collective-permute-start.10
  124.0 17.9 %collective-permute-done.7 = bf16[256,3072]{1,0:T(8,128)(2,1)} collective-permute-done((bf16[256,3072]{1,0:T(8,128)(2,1)S(1)}, bf16[256,3072]{1,0:T(8,128)(2,1)}, u32[]{:S(2)}, u32[]{:S(2)}) %collective-permute-start.7) | collective-permute-done | bytes 1572896 | tf_op jit(solution)/shard_map/ppermute | solution.py:28
  142.4 9.9 %fusion.47.refs_4_ = bf16[512,2048]{1,0:T(8,128)(2,1)S(1)} fusion(bf16[512,3072]{1,0:T(8,128)(2,1)S(1)} %copy-done.29, bf16[2,2048,3072]{2,1,0:T(8,128)(2,1)} %refs_1_.3), kind=kOutput, calls=%fused_computation.68 | convolution fusion | flops 6443499520 | bytes 17825792 | tf_op jit(solution)/shard_map/dot_general | solution.py:57
  154.0 10.8 %fusion.50.refs_4_ = bf16[512,2048]{1,0:T(8,128)(2,1)S(1)} fusion(bf16[512,3072]{1,0:T(8,128)(2,1)S(1)} %constant_dynamic-update-slice_fusion.2.bf_ref, bf16[2,2048,3072]{2,1,0:T(8,128)(2,1)} %refs_1_.3), kind=kOutput, calls=%fused_computation.69 | convolution fusion | flops 6443499520 | bytes 17825792 | tf_op jit(solution)/shard_map/dot_general | solution.py:57
  164.9 2.6 fusion.68.df_ref
  167.5 2.5 convert_add_fusion
  170.1 5.5 collective-permute-done.9
  175.6 32.9 %collective-permute-done.10 = f32[256,1536]{1,0:T(8,128)S(1)} collective-permute-done((f32[256,1536]{1,0:T(8,128)}, f32[256,1536]{1,0:T(8,128)S(1)}, u32[]{:S(2)}, u32[]{:S(2)}) %collective-permute-start.10) | collective-permute-done | bytes 1572896 | tf_op jit(solution)/shard_map/ppermute | solution.py:28
  208.5 2.0 fusion.42
  211.0 1.8 collective-permute-start.12
  214.4 7.5 %fusion.59.qn_ref = bf16[512,1280]{1,0:T(8,128)(2,1)S(1)} fusion(bf16[2,3072,1280]{2,1,0:T(8,128)(2,1)} %refs_3_.21, bf16[256,3072]{1,0:T(8,128)(2,1)S(1)} %collective-permute-done.11, bf16[256,3072]{1,0:T(8,128)(2,1)S(1)} %fusion.35), kind=kOutput, calls=%fused_computation.72 | convolution fusion | flops 4033478656 | bytes 12320768 | tf_op jit(solution)/shard_map/dot_general | solution.py:53
  222.1 19.6 %shard_map.140 = (bf16[512,2048]{1,0:T(8,128)(2,1)}, bf16[512,2048]{1,0:T(8,128)(2,1)}, bf16[512,2048]{1,0:T(8,128)(2,1)}) custom-call(bf16[512,3072]{1,0:T(8,128)(2,1)S(1)} %pad_maximum_fusion.2.refs_0_.refs_1_.an_ref, bf16[512,3072]{1,0:T(8,128)(2,1)S(1)} %pad_maximum_fusion.2.refs_0_.refs_1_.an_ref, bf16[2,3072,2048]{2,1,0:T(8,128)(2,1)} %refs_4_.7, ...), custom_call_target="tpu_custom_call" | custom-call | flops 12884901888 | bytes 35651584 | tf_op jit(solution)/shard_map/pallas_call | solution.py:222
  241.7 6.1 collective-permute-done.12
  247.9 3.3 collective-permute-done.13
  251.4 7.1 %fusion.62.qf_ref = bf16[512,1280]{1,0:T(8,128)(2,1)S(1)} fusion(bf16[512,3072]{1,0:T(8,128)(2,1)S(1)} %constant_dynamic-update-slice_fusion.4.refs_0_.refs_1_.af_ref, bf16[2,3072,1280]{2,1,0:T(8,128)(2,1)} %refs_3_.21), kind=kOutput, calls=%fused_computation.73 | convolution fusion | flops 4027187200 | bytes 12320768 | tf_op jit(solution)/shard_map/dot_general | solution.py:53
  258.5 19.7 %shard_map.141 = (bf16[512,2048]{1,0:T(8,128)(2,1)}, bf16[512,2048]{1,0:T(8,128)(2,1)}, bf16[512,2048]{1,0:T(8,128)(2,1)}) custom-call(bf16[512,3072]{1,0:T(8,128)(2,1)S(1)} %constant_dynamic-update-slice_fusion.4.refs_0_.refs_1_.af_ref, bf16[512,3072]{1,0:T(8,128)(2,1)S(1)} %constant_dynamic-update-slice_fusion.4.refs_0_.refs_1_.af_ref, ...), custom_call_target="tpu_custom_call" | custom-call | flops 12884901888 | bytes 35651584 | tf_op jit(solution)/shard_map/pallas_call | solution.py:222
  278.1 14.0 %attn_fwd.3 = (bf16[1024,1280]{1,0:T(8,128)(2,1)}, bf16[512,768]{1,0:T(8,128)(2,1)S(1)}, bf16[512,768]{1,0:T(8,128)(2,1)S(1)}, f32[2,8,1024]{2,1,0:T(8,128)S(1)}) custom-call(s32[4]{0:T(128)S(1)} %iota_xor_fusion.base_ref, bf16[512,1280]{1,0:T(8,128)(2,1)S(1)} %fusion.59.qn_ref, bf16[512,1280]{1,0:T(8,128)(2,1)S(1)} %fusion.62.qf_ref, ...), custom_call_target="tpu_custom_call" | custom-call | flops 8000000000 | bytes 8000000 | tf_op jit(solution)/shard_map/attn_fwd/pallas_call | solution.py:107
  293.9 16.8 %attn_bwd.2 = (bf16[512,1280]{1,0:T(8,128)(2,1)S(1)}, bf16[512,1280]{1,0:T(8,128)(2,1)S(1)}) custom-call(s32[4]{0:T(128)S(1)} %iota_xor_fusion.base_ref, bf16[1024,1280]{1,0:T(8,128)(2,1)S(1)} %copy-done.44, f32[2,8,1024]{2,1,0:T(8,128)S(1)} %get-tuple-element.136.lse_ref, bf16[512,768]{1,0:T(8,128)(2,1)S(1)} %copy-done.39, ...), custom_call_target="tpu_custom_call" | custom-call | flops 20000000000 | bytes 8000000 | tf_op jit(solution)/shard_map/attn_bwd/pallas_call | solution.py:164
  310.7 22.4 %shard_map.142 = (f32[256,3072]{1,0:T(8,128)S(1)}, f32[256,3072]{1,0:T(8,128)}) custom-call(bf16[512,1280]{1,0:T(8,128)(2,1)S(1)} %get-tuple-element.140.refs_0_.bf_ref, bf16[512,2048]{1,0:T(8,128)(2,1)S(1)} %copy-done.17, bf16[512,2048]{1,0:T(8,128)(2,1)S(1)} %copy-done.18, bf16[2,3072,1280]{2,1,0:T(8,128)(2,1)} %refs_3_.21, ...), custom_call_target="tpu_custom_call" | custom-call | flops 16911433728 | bytes 44826624 | tf_op jit(solution)/shard_map/pallas_call | solution.py:222
  333.3 1.9 copy-done.30
  335.2 6.8 %shard_map.143.rest_0_ = bf16[2,768,3072]{2,1,0:T(8,128)(2,1)} custom-call(bf16[512,768]{1,0:T(8,128)(2,1)S(1)} %get-tuple-element.144.an_ref, bf16[512,768]{1,0:T(8,128)(2,1)S(1)} %get-tuple-element.145.af_ref, bf16[512,3072]{1,0:T(8,128)(2,1)S(1)} %copy-done.30, bf16[512,3072]{1,0:T(8,128)(2,1)S(1)} %copy-done.26), custom_call_target="tpu_custom_call" | custom-call | flops 4831838208 | bytes 12582912 | tf_op jit(solution)/shard_map/pallas_call | solution.py:190
  342.0 2.1 add.74
  344.1 1.7 collective-permute-start.16
  345.9 21.5 %shard_map.144 = (f32[256,3072]{1,0:T(8,128)S(1)}, f32[256,3072]{1,0:T(8,128)S(1)}) custom-call(bf16[512,1280]{1,0:T(8,128)(2,1)S(1)} %get-tuple-element.148.refs_0_.bn_ref, bf16[512,2048]{1,0:T(8,128)(2,1)S(1)} %copy-done.15, bf16[512,2048]{1,0:T(8,128)(2,1)S(1)} %copy-done.16, bf16[2,3072,1280]{2,1,0:T(8,128)(2,1)} %refs_3_.21, ...), custom_call_target="tpu_custom_call" | custom-call | flops 16911433728 | bytes 44826624 | tf_op jit(solution)/shard_map/pallas_call | solution.py:222
  367.5 16.1 %shard_map.147.rest_0_ = bf16[2,3072,2048]{2,1,0:T(8,128)(2,1)} custom-call(bf16[512,3072]{1,0:T(8,128)(2,1)S(1)} %pad_maximum_fusion.2.refs_0_.refs_1_.an_ref, bf16[512,3072]{1,0:T(8,128)(2,1)S(1)} %constant_dynamic-update-slice_fusion.4.refs_0_.refs_1_.af_ref, bf16[512,2048]{1,0:T(8,128)(2,1)S(1)} %copy-done.16, bf16[512,2048]{1,0:T(8,128)(2,1)S(1)} %copy-done.18), custom_call_target="tpu_custom_call" | custom-call | flops 12884901888 | bytes 23068672 | tf_op jit(solution)/shard_map/pallas_call | solution.py:190
  383.6 16.2 %shard_map.146.rest_0_ = bf16[2,3072,2048]{2,1,0:T(8,128)(2,1)} custom-call(bf16[512,3072]{1,0:T(8,128)(2,1)S(1)} %pad_maximum_fusion.2.refs_0_.refs_1_.an_ref, bf16[512,3072]{1,0:T(8,128)(2,1)S(1)} %constant_dynamic-update-slice_fusion.4.refs_0_.refs_1_.af_ref, bf16[512,2048]{1,0:T(8,128)(2,1)S(1)} %copy-done.15, bf16[512,2048]{1,0:T(8,128)(2,1)S(1)} %copy-done.17), custom_call_target="tpu_custom_call" | custom-call | flops 12884901888 | bytes 23068672 | tf_op jit(solution)/shard_map/pallas_call | solution.py:190
  399.8 11.0 %shard_map.145.rest_0_ = bf16[2,3072,1280]{2,1,0:T(8,128)(2,1)} custom-call(bf16[512,3072]{1,0:T(8,128)(2,1)S(1)} %pad_maximum_fusion.2.refs_0_.refs_1_.an_ref, bf16[512,3072]{1,0:T(8,128)(2,1)S(1)} %constant_dynamic-update-slice_fusion.4.refs_0_.refs_1_.af_ref, bf16[512,1280]{1,0:T(8,128)(2,1)S(1)} %get-tuple-element.148.refs_0_.bn_ref, ...), custom_call_target="tpu_custom_call" | custom-call | flops 8053063680 | bytes 16777216 | tf_op jit(solution)/shard_map/pallas_call | solution.py:190
  410.8 3.9 collective-permute-done.16
  414.7 4.3 fusion.36
  420.3 1.8 collective-permute-start.18
  422.5 16.5 %shard_map.148.rest_0_ = bf16[2,2048,3072]{2,1,0:T(8,128)(2,1)} custom-call(bf16[512,2048]{1,0:T(8,128)(2,1)S(1)} %copy-done.37, bf16[512,2048]{1,0:T(8,128)(2,1)S(1)} %copy-done.38, bf16[512,3072]{1,0:T(8,128)(2,1)S(1)} %copy-done.31, bf16[512,3072]{1,0:T(8,128)(2,1)S(1)} %copy-done.27), custom_call_target="tpu_custom_call" | custom-call | flops 12884901888 | bytes 23068672 | tf_op jit(solution)/shard_map/pallas_call | solution.py:190
  440.5 12.7 %shard_map.149 = (bf16[512,2048]{1,0:T(8,128)(2,1)S(1)}, bf16[512,2048]{1,0:T(8,128)(2,1)S(1)}, bf16[512,2048]{1,0:T(8,128)(2,1)S(1)}) custom-call(bf16[512,3072]{1,0:T(8,128)(2,1)S(1)} %constant_dynamic-update-slice_fusion.6.refs_0_.bn_ref, bf16[2,2048,3072]{2,1,0:T(8,128)(2,1)} %refs_1_.3, bf16[512,2048]{1,0:T(8,128)(2,1)S(1)} %copy-done.11, ...), custom_call_target="tpu_custom_call" | custom-call | flops 6442450944 | bytes 19922944 | tf_op jit(solution)/shard_map/pallas_call | solution.py:222
  458.3 3.6 fusion.71.dn_ref
  462.0 3.6 fusion.74.df_ref
  465.6 12.4 %shard_map.150 = (bf16[512,2048]{1,0:T(8,128)(2,1)S(1)}, bf16[512,2048]{1,0:T(8,128)(2,1)S(1)}, bf16[512,2048]{1,0:T(8,128)(2,1)S(1)}) custom-call(bf16[512,3072]{1,0:T(8,128)(2,1)S(1)} %constant_dynamic-update-slice_fusion.8.refs_0_.bf_ref, bf16[2,2048,3072]{2,1,0:T(8,128)(2,1)} %refs_1_.3, bf16[512,2048]{1,0:T(8,128)(2,1)S(1)} %copy-done.13, ...), custom_call_target="tpu_custom_call" | custom-call | flops 6442450944 | bytes 19922944 | tf_op jit(solution)/shard_map/pallas_call | solution.py:222
  479.4 16.9 %attn_bwd.3 = (bf16[512,1280]{1,0:T(8,128)(2,1)S(1)}, bf16[512,1280]{1,0:T(8,128)(2,1)S(1)}) custom-call(s32[4]{0:T(128)S(1)} %iota_xor_fusion.base_ref, bf16[1024,1280]{1,0:T(8,128)(2,1)S(1)} %copy-done.43, f32[2,8,1024]{2,1,0:T(8,128)S(1)} %get-tuple-element.156.lse_ref, bf16[512,768]{1,0:T(8,128)(2,1)S(1)} %copy-done.40, bf16[512,768]{1,0:T(8,128)(2,1)S(1)} %copy-done.41, ...), custom_call_target="tpu_custom_call" | custom-call | flops 20000000000 | bytes 8000000 | tf_op jit(solution)/shard_map/attn_bwd/pallas_call | solution.py:164
  496.3 22.4 %shard_map.151 = (f32[256,3072]{1,0:T(8,128)S(1)}, f32[256,3072]{1,0:T(8,128)}) custom-call(bf16[512,1280]{1,0:T(8,128)(2,1)S(1)} %get-tuple-element.164.refs_0_.bf_ref, bf16[512,2048]{1,0:T(8,128)(2,1)S(1)} %get-tuple-element.167.refs_1_.bf_ref, bf16[512,2048]{1,0:T(8,128)(2,1)S(1)} %get-tuple-element.168.refs_2_.bf_ref, bf16[2,3072,1280]{2,1,0:T(8,128)(2,1)} %refs_3_.21, ...), custom_call_target="tpu_custom_call" | custom-call | flops 16911433728 | bytes 44826624 | tf_op jit(solution)/shard_map/pallas_call | solution.py:222
  520.9 6.8 %shard_map.152 = bf16[2,768,3072]{2,1,0:T(8,128)(2,1)} custom-call(bf16[512,768]{1,0:T(8,128)(2,1)S(1)} %copy-done.10, bf16[512,768]{1,0:T(8,128)(2,1)S(1)} %copy-done.6, bf16[512,3072]{1,0:T(8,128)(2,1)S(1)} %constant_dynamic-update-slice_fusion.6.refs_0_.bn_ref, ...), custom_call_target="tpu_custom_call", output_to_operand_aliasing={{}: (4, {})} | custom-call | flops 4831838208 | bytes 12582912 | tf_op jit(solution)/shard_map/pallas_call | solution.py:190
  529.8 16.3 %shard_map.157 = bf16[2,2048,3072]{2,1,0:T(8,128)(2,1)} custom-call(bf16[512,2048]{1,0:T(8,128)(2,1)S(1)} %copy-done.20, bf16[512,2048]{1,0:T(8,128)(2,1)S(1)} %copy-done.22, bf16[512,3072]{1,0:T(8,128)(2,1)S(1)} %constant_dynamic-update-slice_fusion.6.refs_0_.bn_ref, ...), custom_call_target="tpu_custom_call", output_to_operand_aliasing={{}: (4, {})} | custom-call | flops 12884901888 | bytes 23068672 | tf_op jit(solution)/shard_map/pallas_call | solution.py:190
  547.6 4.3 add.78
  552.2 21.5 %shard_map.153 = (f32[256,3072]{1,0:T(8,128)S(1)}, f32[256,3072]{1,0:T(8,128)S(1)}) custom-call(bf16[512,1280]{1,0:T(8,128)(2,1)S(1)} %get-tuple-element.173.refs_0_.bn_ref, bf16[512,2048]{1,0:T(8,128)(2,1)S(1)} %get-tuple-element.174.refs_1_.bn_ref, bf16[512,2048]{1,0:T(8,128)(2,1)S(1)} %get-tuple-element.175.refs_2_.bn_ref, ...), custom_call_target="tpu_custom_call" | custom-call | flops 16911433728 | bytes 44826624 | tf_op jit(solution)/shard_map/pallas_call | solution.py:222
  573.7 16.3 %shard_map.155 = bf16[2,3072,2048]{2,1,0:T(8,128)(2,1)} custom-call(bf16[512,3072]{1,0:T(8,128)(2,1)S(1)} %constant_dynamic-update-slice_fusion.10.an_ref, bf16[512,3072]{1,0:T(8,128)(2,1)S(1)} %constant_dynamic-update-slice_fusion.12.af_ref, bf16[512,2048]{1,0:T(8,128)(2,1)S(1)} %get-tuple-element.174.refs_1_.bn_ref, ...), custom_call_target="tpu_custom_call", output_to_operand_aliasing={{}: (4, {})} | custom-call | flops 12884901888 | bytes 23068672 | tf_op jit(solution)/shard_map/pallas_call | solution.py:190
  590.0 16.2 %shard_map.156 = bf16[2,3072,2048]{2,1,0:T(8,128)(2,1)} custom-call(bf16[512,3072]{1,0:T(8,128)(2,1)S(1)} %constant_dynamic-update-slice_fusion.10.an_ref, bf16[512,3072]{1,0:T(8,128)(2,1)S(1)} %constant_dynamic-update-slice_fusion.12.af_ref, bf16[512,2048]{1,0:T(8,128)(2,1)S(1)} %get-tuple-element.175.refs_2_.bn_ref, ...), custom_call_target="tpu_custom_call", output_to_operand_aliasing={{}: (4, {})} | custom-call | flops 12884901888 | bytes 23068672 | tf_op jit(solution)/shard_map/pallas_call | solution.py:190
  606.2 11.2 %shard_map.154 = bf16[2,3072,1280]{2,1,0:T(8,128)(2,1)} custom-call(bf16[512,3072]{1,0:T(8,128)(2,1)S(1)} %constant_dynamic-update-slice_fusion.10.an_ref, bf16[512,3072]{1,0:T(8,128)(2,1)S(1)} %constant_dynamic-update-slice_fusion.12.af_ref, bf16[512,1280]{1,0:T(8,128)(2,1)S(1)} %get-tuple-element.173.refs_0_.bn_ref, ...), custom_call_target="tpu_custom_call", output_to_operand_aliasing={{}: (4, {})} | custom-call | flops 8053063680 | bytes 16777216 | tf_op jit(solution)/shard_map/pallas_call | solution.py:190
  617.5 4.9 collective-permute-done.25
  622.5 3.7 fusion.37
  627.8 2.4 fusion.41
  (225 shorter events, 34.1 us)
Async XLA Ops:
  0.6 9.4 %collective-permute-start.1 = (bf16[256,3072]{1,0:T(8,128)(2,1)}, bf16[256,3072]{1,0:T(8,128)(2,1)S(1)}, u32[]{:S(2)}, u32[]{:S(2)}) collective-permute-start(bf16[256,3072]{1,0:T(8,128)(2,1)} %param.9), channel_id=1, source_target_pairs={{0,1},{1,0},{2,3},{3,2},{4,5},{5,4},{6,7},{7,6}} | collective-permute-start | bytes 4718600 | tf_op jit(solution)/shard_map/ppermute | solution.py:24
  6.8 15.5 %copy-start.50 = (bf16[256,3072]{1,0:T(8,128)(2,1)}, bf16[256,3072]{1,0:T(8,128)(2,1)S(1)}, u32[]{:S(2)}) copy-start(bf16[256,3072]{1,0:T(8,128)(2,1)S(1)} %fusion.34) | copy-start | bytes 4718596
  6.8 6.8 %collective-permute-start = (bf16[256,3072]{1,0:T(8,128)(2,1)S(1)}, bf16[256,3072]{1,0:T(8,128)(2,1)S(1)}, u32[]{:S(2)}, u32[]{:S(2)}) collective-permute-start(bf16[256,3072]{1,0:T(8,128)(2,1)S(1)} %fusion.34), channel_id=1, source_target_pairs={{0,1},{1,0},{2,3},{3,2},{4,5},{5,4},{6,7},{7,6}} | collective-permute-start | bytes 4718600 | tf_op jit(solution)/shard_map/ppermute | solution.py:24
  6.9 37.6 %collective-permute-start.2 = (bf16[256,3072]{1,0:T(8,128)(2,1)S(1)}, bf16[256,3072]{1,0:T(8,128)(2,1)}, u32[]{:S(2)}, u32[]{:S(2)}) collective-permute-start(bf16[256,3072]{1,0:T(8,128)(2,1)S(1)} %fusion.34), channel_id=1, source_target_pairs={{0,2},{2,0},{1,3},{3,1},{4,6},{6,4},{5,7},{7,5}} | collective-permute-start | bytes 4718600 | tf_op jit(solution)/shard_map/ppermute | solution.py:28
  44.6 3.8 collective-permute-start.3
  46.9 28.6 %copy-start.32 = (f32[1024,128]{1,0:T(8,128)}, f32[1024,128]{1,0:T(8,128)S(1)}, u32[]{:S(2)}) copy-start(f32[1024,128]{1,0:T(8,128)S(1)} %get-tuple-element.208.cos_ref) | copy-start | bytes 1572868
  46.9 28.6 %copy-start.34 = (f32[1024,128]{1,0:T(8,128)}, f32[1024,128]{1,0:T(8,128)S(1)}, u32[]{:S(2)}) copy-start(f32[1024,128]{1,0:T(8,128)S(1)} %get-tuple-element.209.sin_ref) | copy-start | bytes 1572868
  57.1 18.4 %copy-start.42 = (bf16[512,1280]{1,0:T(8,128)(2,1)S(1)}, bf16[512,1280]{1,0:T(8,128)(2,1)}, u32[]{:S(2)}) copy-start(bf16[512,1280]{1,0:T(8,128)(2,1)} %fusion.53.qn_ref) | copy-start | bytes 3932164
  75.5 14.2 %slice-start = ((s8[9437184]{0:T(1024)(128)(4,1)}), s8[4194304]{0:T(1024)(128)(4,1)S(1)}, s32[]{:S(2)}) async-start(s8[9437184]{0:T(1024)(128)(4,1)} %bitcast.57), calls=%async_computation | async-start | bytes 8388608
  75.5 14.2 %slice-start.1 = ((s8[9437184]{0:T(1024)(128)(4,1)}), s8[4194304]{0:T(1024)(128)(4,1)S(1)}, s32[]{:S(2)}) async-start(s8[9437184]{0:T(1024)(128)(4,1)} %bitcast.57), calls=%async_computation.1 | async-start | bytes 8388608
  75.5 14.2 %slice-start.2 = ((s8[9437184]{0:T(1024)(128)(4,1)}), s8[1048576]{0:T(1024)(128)(4,1)S(1)}, s32[]{:S(2)}) async-start(s8[9437184]{0:T(1024)(128)(4,1)} %bitcast.57), calls=%async_computation.2 | async-start | bytes 2097152
  89.7 18.3 %copy-start.9 = (bf16[512,768]{1,0:T(8,128)(2,1)}, bf16[512,768]{1,0:T(8,128)(2,1)S(1)}, u32[]{:S(2)}) copy-start(bf16[512,768]{1,0:T(8,128)(2,1)S(1)} %get-tuple-element.115.refs_0_.an_ref) | copy-start | bytes 2359300
  97.1 9.2 %collective-permute-start.5 = (f32[256,1536]{1,0:T(8,128)S(1)}, f32[256,1536]{1,0:T(8,128)S(1)}, u32[]{:S(2)}, u32[]{:S(2)}) collective-permute-start(f32[256,1536]{1,0:T(8,128)S(1)} %get-tuple-element.107), channel_id=1, source_target_pairs={{0,1},{1,0},{2,3},{3,2},{4,5},{5,4},{6,7},{7,6}} | collective-permute-start | bytes 4718600 | tf_op jit(solution)/shard_map/ppermute | solution.py:24
  104.2 16.7 %collective-permute-start.4 = (f32[256,1536]{1,0:T(8,128)S(1)}, f32[256,1536]{1,0:T(8,128)S(1)}, u32[]{:S(2)}, u32[]{:S(2)}) collective-permute-start(f32[256,1536]{1,0:T(8,128)S(1)} %get-tuple-element.109), channel_id=1, source_target_pairs={{0,1},{1,0},{2,3},{3,2},{4,5},{5,4},{6,7},{7,6}} | collective-permute-start | bytes 4718600 | tf_op jit(solution)/shard_map/ppermute | solution.py:24
  104.5 37.4 %collective-permute-start.7 = (bf16[256,3072]{1,0:T(8,128)(2,1)S(1)}, bf16[256,3072]{1,0:T(8,128)(2,1)}, u32[]{:S(2)}, u32[]{:S(2)}) collective-permute-start(bf16[256,3072]{1,0:T(8,128)(2,1)S(1)} %copy-done.55), channel_id=1, source_target_pairs={{0,2},{2,0},{1,3},{3,1},{4,6},{6,4},{5,7},{7,5}} | collective-permute-start | bytes 4718600 | tf_op jit(solution)/shard_map/ppermute | solution.py:28
  107.7 67.9 %collective-permute-start.9 = (f32[256,1536]{1,0:T(8,128)}, f32[256,1536]{1,0:T(8,128)}, u32[]{:S(2)}, u32[]{:S(2)}) collective-permute-start(f32[256,1536]{1,0:T(8,128)} %add.68), channel_id=1, source_target_pairs={{0,2},{2,0},{1,3},{3,1},{4,6},{6,4},{5,7},{7,5}} | collective-permute-start | bytes 4718600 | tf_op jit(solution)/shard_map/ppermute | solution.py:28
  120.9 21.6 %copy-start.29 = (bf16[512,3072]{1,0:T(8,128)(2,1)S(1)}, bf16[512,3072]{1,0:T(8,128)(2,1)}, u32[]{:S(2)}) copy-start(bf16[512,3072]{1,0:T(8,128)(2,1)} %copy-done.28) | copy-start | bytes 9437188
  122.2 86.2 %collective-permute-start.10 = (f32[256,1536]{1,0:T(8,128)}, f32[256,1536]{1,0:T(8,128)S(1)}, u32[]{:S(2)}, u32[]{:S(2)}) collective-permute-start(f32[256,1536]{1,0:T(8,128)} %add.71), channel_id=1, source_target_pairs={{0,2},{2,0},{1,3},{3,1},{4,6},{6,4},{5,7},{7,5}} | collective-permute-start | bytes 4718600 | tf_op jit(solution)/shard_map/ppermute | solution.py:28
  141.9 12.0 %collective-permute-start.8 = (bf16[256,3072]{1,0:T(8,128)(2,1)}, bf16[256,3072]{1,0:T(8,128)(2,1)S(1)}, u32[]{:S(2)}, u32[]{:S(2)}) collective-permute-start(bf16[256,3072]{1,0:T(8,128)(2,1)} %collective-permute-done.7), channel_id=1, source_target_pairs={{0,1},{1,0},{2,3},{3,2},{4,5},{5,4},{6,7},{7,6}} | collective-permute-start | bytes 4718600 | tf_op jit(solution)/shard_map/ppermute | solution.py:24
  141.9 25.6 %collective-permute-start.6 = (f32[256,3072]{1,0:T(8,128)}, f32[256,3072]{1,0:T(8,128)}, u32[]{:S(2)}, u32[]{:S(2)}) collective-permute-start(f32[256,3072]{1,0:T(8,128)} %get-tuple-element.119), channel_id=1, source_target_pairs={{0,1},{1,0},{2,3},{3,2},{4,5},{5,4},{6,7},{7,6}} | collective-permute-start | bytes 9437192 | tf_op jit(solution)/shard_map/ppermute | solution.py:24
  170.1 40.4 %copy-start.59 = (f32[1,3072]{1,0:T(1,128)S(1)}, f32[1,3072]{1,0:T(1,128)}, u32[]{:S(2)}) copy-start(f32[1,3072]{1,0:T(1,128)} %get-tuple-element.203) | copy-start | bytes 36868
  211.0 3.4 collective-permute-start.11
  211.0 36.8 %collective-permute-start.12 = (bf16[256,3072]{1,0:T(8,128)(2,1)S(1)}, bf16[256,3072]{1,0:T(8,128)(2,1)S(1)}, u32[]{:S(2)}, u32[]{:S(2)}) collective-permute-start(bf16[256,3072]{1,0:T(8,128)(2,1)S(1)} %fusion.35), channel_id=1, source_target_pairs={{0,2},{2,0},{1,3},{3,1},{4,6},{6,4},{5,7},{7,5}} | collective-permute-start | bytes 4718600 | tf_op jit(solution)/shard_map/ppermute | solution.py:28
  247.8 3.4 collective-permute-start.13
  258.4 19.7 %copy-start.33 = (f32[1024,128]{1,0:T(8,128)S(1)}, f32[1024,128]{1,0:T(8,128)}, u32[]{:S(2)}) copy-start(f32[1024,128]{1,0:T(8,128)} %copy-done.32) | copy-start | bytes 1572868
  258.4 19.7 %copy-start.35 = (f32[1024,128]{1,0:T(8,128)S(1)}, f32[1024,128]{1,0:T(8,128)}, u32[]{:S(2)}) copy-start(f32[1024,128]{1,0:T(8,128)} %copy-done.34) | copy-start | bytes 1572868
  278.1 14.0 %copy-start.39 = (bf16[512,768]{1,0:T(8,128)(2,1)S(1)}, bf16[512,768]{1,0:T(8,128)(2,1)}, u32[]{:S(2)}) copy-start(bf16[512,768]{1,0:T(8,128)(2,1)} %fusion.65.dn_ref) | copy-start | bytes 2359300
  293.9 16.9 %copy-start.17 = (bf16[512,2048]{1,0:T(8,128)(2,1)S(1)}, bf16[512,2048]{1,0:T(8,128)(2,1)}, u32[]{:S(2)}) copy-start(bf16[512,2048]{1,0:T(8,128)(2,1)} %get-tuple-element.141.refs_1_.bf_ref) | copy-start | bytes 6291460
  293.9 16.9 %copy-start.18 = (bf16[512,2048]{1,0:T(8,128)(2,1)S(1)}, bf16[512,2048]{1,0:T(8,128)(2,1)}, u32[]{:S(2)}) copy-start(bf16[512,2048]{1,0:T(8,128)(2,1)} %get-tuple-element.142.refs_2_.bf_ref) | copy-start | bytes 6291460
  310.7 22.4 %copy-start.23 = (bf16[512,1280]{1,0:T(8,128)(2,1)}, bf16[512,1280]{1,0:T(8,128)(2,1)S(1)}, u32[]{:S(2)}) copy-start(bf16[512,1280]{1,0:T(8,128)(2,1)S(1)} %get-tuple-element.140.refs_0_.bf_ref) | copy-start | bytes 3932164
  310.7 22.6 %copy-start.26 = (bf16[512,3072]{1,0:T(8,128)(2,1)S(1)}, bf16[512,3072]{1,0:T(8,128)(2,1)}, u32[]{:S(2)}) copy-start(bf16[512,3072]{1,0:T(8,128)(2,1)} %copy-done.25) | copy-start | bytes 9437188
  333.1 8.8 %collective-permute-start.14 = (f32[256,3072]{1,0:T(8,128)}, f32[256,3072]{1,0:T(8,128)S(1)}, u32[]{:S(2)}, u32[]{:S(2)}) collective-permute-start(f32[256,3072]{1,0:T(8,128)} %get-tuple-element.146), channel_id=1, source_target_pairs={{0,1},{1,0},{2,3},{3,2},{4,5},{5,4},{6,7},{7,6}} | collective-permute-start | bytes 9437192 | tf_op jit(solution)/shard_map/ppermute | solution.py:24
  344.1 70.6 %collective-permute-start.16 = (f32[256,3072]{1,0:T(8,128)}, f32[256,3072]{1,0:T(8,128)S(1)}, u32[]{:S(2)}, u32[]{:S(2)}) collective-permute-start(f32[256,3072]{1,0:T(8,128)} %add.74), channel_id=1, source_target_pairs={{0,2},{2,0},{1,3},{3,1},{4,6},{6,4},{5,7},{7,5}} | collective-permute-start | bytes 9437192 | tf_op jit(solution)/shard_map/ppermute | solution.py:28
  367.4 47.3 %collective-permute-start.15 = (f32[256,3072]{1,0:T(8,128)S(1)}, f32[256,3072]{1,0:T(8,128)}, u32[]{:S(2)}, u32[]{:S(2)}) collective-permute-start(f32[256,3072]{1,0:T(8,128)S(1)} %get-tuple-element.152), channel_id=1, source_target_pairs={{0,1},{1,0},{2,3},{3,2},{4,5},{5,4},{6,7},{7,6}} | collective-permute-start | bytes 9437192 | tf_op jit(solution)/shard_map/ppermute | solution.py:24
  383.6 16.2 %copy-start.24 = (bf16[512,1280]{1,0:T(8,128)(2,1)S(1)}, bf16[512,1280]{1,0:T(8,128)(2,1)}, u32[]{:S(2)}) copy-start(bf16[512,1280]{1,0:T(8,128)(2,1)} %copy-done.23) | copy-start | bytes 3932164
  399.8 14.9 %copy-start.49 = (bf16[256,3072]{1,0:T(8,128)(2,1)S(1)}, bf16[256,3072]{1,0:T(8,128)(2,1)}, u32[]{:S(2)}) copy-start(bf16[256,3072]{1,0:T(8,128)(2,1)} %copy-done.48) | copy-start | bytes 4718596
  399.8 14.9 %copy-start.60 = (f32[1,3072]{1,0:T(1,128)S(1)}, f32[1,3072]{1,0:T(1,128)}, u32[]{:S(2)}) copy-start(f32[1,3072]{1,0:T(1,128)} %get-tuple-element.203) | copy-start | bytes 36868
  399.8 14.9 %copy-start.65 = (f32[256]{0:T(256)S(1)}, f32[256]{0:T(256)}, u32[]{:S(2)}) copy-start(f32[256]{0:T(256)} %copy-done.64) | copy-start | bytes 3076
  420.3 18.6 %copy-start.52 = (bf16[256,3072]{1,0:T(8,128)(2,1)}, bf16[256,3072]{1,0:T(8,128)(2,1)S(1)}, u32[]{:S(2)}) copy-start(bf16[256,3072]{1,0:T(8,128)(2,1)S(1)} %fusion.39) | copy-start | bytes 4718596
  420.3 35.8 %collective-permute-start.18 = (bf16[256,3072]{1,0:T(8,128)(2,1)S(1)}, bf16[256,3072]{1,0:T(8,128)(2,1)S(1)}, u32[]{:S(2)}, u32[]{:S(2)}) collective-permute-start(bf16[256,3072]{1,0:T(8,128)(2,1)S(1)} %fusion.39), channel_id=1, source_target_pairs={{0,2},{2,0},{1,3},{3,1},{4,6},{6,4},{5,7},{7,5}} | collective-permute-start | bytes 4718600 | tf_op jit(solution)/shard_map/ppermute | solution.py:28
  422.1 16.9 %collective-permute-start.17 = (bf16[256,3072]{1,0:T(8,128)(2,1)S(1)}, bf16[256,3072]{1,0:T(8,128)(2,1)S(1)}, u32[]{:S(2)}, u32[]{:S(2)}) collective-permute-start(bf16[256,3072]{1,0:T(8,128)(2,1)S(1)} %fusion.39), channel_id=1, source_target_pairs={{0,1},{1,0},{2,3},{3,2},{4,5},{5,4},{6,7},{7,6}} | collective-permute-start | bytes 4718600 | tf_op jit(solution)/shard_map/ppermute | solution.py:24
  422.5 16.7 %copy-start.12 = (bf16[512,2048]{1,0:T(8,128)(2,1)S(1)}, bf16[512,2048]{1,0:T(8,128)(2,1)}, u32[]{:S(2)}) copy-start(bf16[512,2048]{1,0:T(8,128)(2,1)} %get-tuple-element.160.refs_3_) | copy-start | bytes 6291460
  438.9 19.3 %slice-start.3 = ((s8[9437184]{0:T(1024)(128)(4,1)}), s8[4194304]{0:T(1024)(128)(4,1)S(1)}, s32[]{:S(2)}) async-start(s8[9437184]{0:T(1024)(128)(4,1)} %bitcast.59), calls=%async_computation.3 | async-start | bytes 8388608
  440.5 15.6 %copy-start.51 = (bf16[256,3072]{1,0:T(8,128)(2,1)S(1)}, bf16[256,3072]{1,0:T(8,128)(2,1)}, u32[]{:S(2)}) copy-start(bf16[256,3072]{1,0:T(8,128)(2,1)} %copy-done.50) | copy-start | bytes 4718596
  440.5 17.7 %slice-start.4 = ((s8[9437184]{0:T(1024)(128)(4,1)}), s8[4194304]{0:T(1024)(128)(4,1)S(1)}, s32[]{:S(2)}) async-start(s8[9437184]{0:T(1024)(128)(4,1)} %bitcast.59), calls=%async_computation.4 | async-start | bytes 8388608
  440.5 17.7 %slice-start.5 = ((s8[9437184]{0:T(1024)(128)(4,1)}), s8[1048576]{0:T(1024)(128)(4,1)S(1)}, s32[]{:S(2)}) async-start(s8[9437184]{0:T(1024)(128)(4,1)} %bitcast.59), calls=%async_computation.5 | async-start | bytes 2097152
  456.1 5.7 collective-permute-start.19
  456.2 63.0 %collective-permute-start.23 = (bf16[256,3072]{1,0:T(8,128)(2,1)S(1)}, bf16[256,3072]{1,0:T(8,128)(2,1)}, u32[]{:S(2)}, u32[]{:S(2)}) collective-permute-start(bf16[256,3072]{1,0:T(8,128)(2,1)S(1)} %copy-done.51), channel_id=1, source_target_pairs={{0,2},{2,0},{1,3},{3,1},{4,6},{6,4},{5,7},{7,5}} | collective-permute-start | bytes 4718600 | tf_op jit(solution)/shard_map/ppermute | solution.py:28
  457.9 69.9 %collective-permute-start.22 = (bf16[256,3072]{1,0:T(8,128)(2,1)S(1)}, bf16[256,3072]{1,0:T(8,128)(2,1)}, u32[]{:S(2)}, u32[]{:S(2)}) collective-permute-start(bf16[256,3072]{1,0:T(8,128)(2,1)S(1)} %copy-done.51), channel_id=1, source_target_pairs={{0,1},{1,0},{2,3},{3,2},{4,5},{5,4},{6,7},{7,6}} | collective-permute-start | bytes 4718600 | tf_op jit(solution)/shard_map/ppermute | solution.py:24
  479.3 16.9 %copy-start.1 = (bf16[512,2048]{1,0:T(8,128)(2,1)}, bf16[512,2048]{1,0:T(8,128)(2,1)S(1)}, u32[]{:S(2)}) copy-start(bf16[512,2048]{1,0:T(8,128)(2,1)S(1)} %get-tuple-element.168.refs_2_.bf_ref) | copy-start | bytes 6291460
  479.3 16.9 %copy-start.3 = (bf16[512,2048]{1,0:T(8,128)(2,1)}, bf16[512,2048]{1,0:T(8,128)(2,1)S(1)}, u32[]{:S(2)}) copy-start(bf16[512,2048]{1,0:T(8,128)(2,1)S(1)} %get-tuple-element.167.refs_1_.bf_ref) | copy-start | bytes 6291460
  496.2 22.5 %copy-start.7 = (bf16[512,1280]{1,0:T(8,128)(2,1)}, bf16[512,1280]{1,0:T(8,128)(2,1)S(1)}, u32[]{:S(2)}) copy-start(bf16[512,1280]{1,0:T(8,128)(2,1)S(1)} %get-tuple-element.164.refs_0_.bf_ref) | copy-start | bytes 3932164
  518.7 28.9 %collective-permute-start.20 = (f32[256,3072]{1,0:T(8,128)}, f32[256,3072]{1,0:T(8,128)}, u32[]{:S(2)}, u32[]{:S(2)}) collective-permute-start(f32[256,3072]{1,0:T(8,128)} %get-tuple-element.171), channel_id=1, source_target_pairs={{0,1},{1,0},{2,3},{3,2},{4,5},{5,4},{6,7},{7,6}} | collective-permute-start | bytes 9437192 | tf_op jit(solution)/shard_map/ppermute | solution.py:24
  519.1 27.0 %collective-permute-start.24 = (bf16[256,3072]{1,0:T(8,128)(2,1)}, bf16[256,3072]{1,0:T(8,128)(2,1)}, u32[]{:S(2)}, u32[]{:S(2)}) collective-permute-start(bf16[256,3072]{1,0:T(8,128)(2,1)} %collective-permute-done.23), channel_id=1, source_target_pairs={{0,1},{1,0},{2,3},{3,2},{4,5},{5,4},{6,7},{7,6}} | collective-permute-start | bytes 4718600 | tf_op jit(solution)/shard_map/ppermute | solution.py:24
  551.9 70.5 %collective-permute-start.25 = (f32[256,3072]{1,0:T(8,128)}, f32[256,3072]{1,0:T(8,128)S(1)}, u32[]{:S(2)}, u32[]{:S(2)}) collective-permute-start(f32[256,3072]{1,0:T(8,128)} %add.78), channel_id=1, source_target_pairs={{0,2},{2,0},{1,3},{3,1},{4,6},{6,4},{5,7},{7,5}} | collective-permute-start | bytes 9437192 | tf_op jit(solution)/shard_map/ppermute | solution.py:28
  552.2 21.5 %copy-start.4 = (bf16[512,2048]{1,0:T(8,128)(2,1)S(1)}, bf16[512,2048]{1,0:T(8,128)(2,1)}, u32[]{:S(2)}) copy-start(bf16[512,2048]{1,0:T(8,128)(2,1)} %copy-done.3) | copy-start | bytes 6291460
  573.7 16.3 %copy-start.2 = (bf16[512,2048]{1,0:T(8,128)(2,1)S(1)}, bf16[512,2048]{1,0:T(8,128)(2,1)}, u32[]{:S(2)}) copy-start(bf16[512,2048]{1,0:T(8,128)(2,1)} %copy-done.1) | copy-start | bytes 6291460
  573.7 48.7 %collective-permute-start.21 = (f32[256,3072]{1,0:T(8,128)S(1)}, f32[256,3072]{1,0:T(8,128)}, u32[]{:S(2)}, u32[]{:S(2)}) collective-permute-start(f32[256,3072]{1,0:T(8,128)S(1)} %get-tuple-element.177), channel_id=1, source_target_pairs={{0,1},{1,0},{2,3},{3,2},{4,5},{5,4},{6,7},{7,6}} | collective-permute-start | bytes 9437192 | tf_op jit(solution)/shard_map/ppermute | solution.py:24
  590.0 16.2 %copy-start.8 = (bf16[512,1280]{1,0:T(8,128)(2,1)S(1)}, bf16[512,1280]{1,0:T(8,128)(2,1)}, u32[]{:S(2)}) copy-start(bf16[512,1280]{1,0:T(8,128)(2,1)} %copy-done.7) | copy-start | bytes 3932164
  606.2 16.2 %copy-start.47 = (bf16[256,3072]{1,0:T(8,128)(2,1)S(1)}, bf16[256,3072]{1,0:T(8,128)(2,1)}, u32[]{:S(2)}) copy-start(bf16[256,3072]{1,0:T(8,128)(2,1)} %param.8) | copy-start | bytes 4718596
  606.2 16.2 %copy-start.58 = (f32[1,3072]{1,0:T(1,128)S(1)}, f32[1,3072]{1,0:T(1,128)}, u32[]{:S(2)}) copy-start(f32[1,3072]{1,0:T(1,128)} %copy-done.57) | copy-start | bytes 36868
  606.2 16.2 %copy-start.63 = (f32[256]{0:T(256)S(1)}, f32[256]{0:T(256)}, u32[]{:S(2)}) copy-start(f32[256]{0:T(256)} %copy-done.62) | copy-start | bytes 3076
  626.2 1.2 collective-permute-start.26
  627.4 3.8 collective-permute-start.27
  (40 other events, 231.8 us)
where the time goes:
time: 638 us; the launch traced here: 632 us
  Pallas kernels  412 us (65%)
  waiting for transfers between devices  84.7 us (13%)
  matrix products  60.6 us (9%)
  other arithmetic  35.2 us (6%)
  local copies, waits for them, and re-layouts  20.7 us (3%)
  starting transfers between devices  17.3 us (3%)
    pallas_call x13, Pallas kernels, fused_mm(): pl.pallas_call(kernel, grid=(steps,), in_specs=in_specs, out_specs=[pl.Bl...  216 us
    pallas_call x10, Pallas kernels, wgrad(): pl.pallas_call(wgrad_kernel, grid=(m_dim // block_rows,), in_specs=in_spe...  133 us
    ppermute x10, waiting for transfers between devices, chip_swap(): return lax.ppermute(values, 'tp', CHIP_PAIRS)  77.1 us
    dot_general x6, matrix products, dot_t(): lax.dot_general(lhs, rhs, (((1,), (1,)), ((), ())), preferred_element_typ...  34.1 us
    pallas_call x2, Pallas kernels, attn_bwd(): pl.pallas_call(attn_bwd_kernel, grid=(groups,), name='attn_bwd', in_specs...  33.7 us
    pallas_call x2, Pallas kernels, attn_fwd(): pl.pallas_call(attn_fwd_kernel, grid=(groups,), name='attn_fwd', in_specs...  28.1 us
    dot_general x4, matrix products, dot(): return jnp.dot(lhs, rhs, preferred_element_type=F32)  26.5 us
    unnamed x159, local copies, waits for them, and re-layouts  15.6 us
  transfers between devices with their start and end apart: 28, of which 13 were waited for; matrix products, arithmetic and copies ran while one was open for 11% of the time, Pallas kernels for 47%

commit v1 on v0

--- a/solution.py
+++ b/solution.py
@@ -1,3 +1,5 @@
+import functools
+
 import jax
 import jax.numpy as jnp
 from jax import lax
@@ -15,6 +17,7 @@
 SCALE = HEAD_DIM ** -0.5
 CORE_PAIRS = [(0, 1), (1, 0), (2, 3), (3, 2)]
 CHIP_PAIRS = [(0, 2), (2, 0), (1, 3), (3, 1)]
+CROSS_PAIRS = [(0, 3), (3, 0), (1, 2), (2, 1)]
 VMEM_LIMIT = 40 << 20
 MM_VMEM = 28 << 20
 WG_VMEM = 36 << 20
@@ -59,6 +62,23 @@
 
 def dot_lt(lhs, rhs):
     return lax.dot_general(lhs, rhs, (((0,), (0,)), ((), ())), preferred_element_type=F32)
+
+
+def norm_kernel(layer, x_ref, gain_ref, dy_ref, u_ref, dy_copy_ref):
+    u_ref[...] = rms_scale(x_ref[...].astype(F32), gain_ref[layer:layer + 1, :]).astype(BF16)
+    dy_copy_ref[...] = dy_ref[...]
+
+
+def norm(x_loc, norm_gain, layer, dy_loc):
+    rows, width = x_loc.shape
+    block = pl.BlockSpec((rows // 4, width), lambda i: (i, 0))
+    return pl.pallas_call(
+        functools.partial(norm_kernel, layer), grid=(4,), name='norm',
+        in_specs=[block, pl.BlockSpec(norm_gain.shape, lambda i: (0, 0)), block], out_specs=[block, block],
+        out_shape=[jax.ShapeDtypeStruct((rows, width), BF16), pltpu.VMEM((rows, width), BF16)],
+        cost_estimate=pl.CostEstimate(flops=6 * rows * width, bytes_accessed=4 * rows * width, transcendentals=rows),
+        compiler_params=pltpu.CompilerParams(vmem_limit_bytes=16 << 20),
+    )(x_loc, norm_gain, dy_loc)
 
 
 def attn_fwd_kernel(base_ref, qn_ref, qf_ref, cos_ref, sin_ref, rq_ref, on_ref, of_ref, lse_ref, o_scr):
@@ -172,27 +192,71 @@
     )(base, rot_qkv, lse, d_halves[0][0], d_halves[1][0], cos_tab, sin_tab)
 
 
-def wgrad_kernel(an_ref, af_ref, bn_ref, bf_ref, *rest):
-    out_ref = rest[-1]
-    out_ref[0] = (dot_lt(an_ref[...], bn_ref[...]) + dot_lt(af_ref[...], bf_ref[...])).astype(BF16)
-
-
-def wgrad(half, lhs, rhs, layer_idx, n_layers, stacked, block_rows):
+def mxu_passes(rows, tiles, emit):
+    def body(*accs):
+        for g, pair in enumerate(tiles):
+            use = accs[2 * (g % (len(accs) // 2)):][:2]
+            for step in range(max(len(t) for t in pair)):
+                for q, tile in enumerate(pair):
+                    lhs, rhs, transposed = tile[step]
+                    pltpu.matmul_push_rhs(rhs(), staging_register=step % 2, mxu_index=q, transpose=transposed)
+                    pltpu.matmul_acc_lhs(use[q], lhs(), load_staged_rhs=step % 2)
+            emit(g, [pltpu.matmul_pop(use[q]) for q in range(2)])
+
+    n_acc = 2 if rows <= 512 else 1
+    pl.run_scoped(body, *[pltpu.ACC(q)((rows, 256), F32) for _ in range(n_acc) for q in range(2)])
+
+
+def wgrad(lhs, rhs, layer_idx, n_layers, stacked, block_rows):
     m_dim, n_dim = lhs[0][0].shape[1], rhs[0][0].shape[1]
-    in_specs = [pl.BlockSpec((half, block_rows), lambda m, r=r: (r, m)) for _, r in lhs]
-    in_specs += [pl.BlockSpec((half, n_dim), lambda m, r=r: (r, 0)) for _, r in rhs]
-    args = [arr for arr, _ in lhs + rhs]
+    n_l, n_r = len(lhs), len(rhs)
+    depth = sum(rows for _, _, rows in lhs)
+
+    def kernel(*refs):
+        out_ref, t_scr = refs[-2:]
+        row = 0
+        for ref, (_, _, rows) in zip(refs, lhs):
+            t_scr[:, row:row + rows] = jnp.transpose(ref[...])
+            row += rows
+        where = [(ref, k) for ref, (_, _, rows) in zip(refs[n_l:n_l + n_r], rhs) for k in range(0, rows, 256)]
+
+        def passes(part, col):
+            def one(k):
+                ref, first = where[k]
+                return lambda: t_scr[part, k * 256:(k + 1) * 256], lambda: ref[first:first + 256, col:col + 256], False
+
+            return [one(k) for k in range(len(where))]
+
+        whole = slice(0, block_rows)
+        halves = [slice(0, block_rows // 2), slice(block_rows // 2, block_rows)]
+
+        def emit(g, accs):
+            for q in range(2):
+                out_ref[0, :, g * 512 + q * 256:g * 512 + q * 256 + 256] = accs[q].astype(BF16)
+
+        def emit_last(g, accs):
+            for q in range(2):
+                out_ref[0, halves[q], n_dim - 256:] = accs[q].astype(BF16)
+
+        mxu_passes(block_rows, [[passes(whole, col), passes(whole, col + 256)] for col in range(0, n_dim - 511, 512)], emit)
+        if n_dim % 512:
+            mxu_passes(block_rows // 2, [[passes(half, n_dim - 256) for half in halves]], emit_last)
+
+    in_specs = [pl.BlockSpec((rows, block_rows), lambda m, r=first // rows: (r, m)) for _, first, rows in lhs]
+    in_specs += [pl.BlockSpec((rows, n_dim), lambda m, r=first // rows: (r, 0)) for _, first, rows in rhs]
+    args = [piece[0] for piece in lhs + rhs]
     aliases = {}
     if stacked is not None:
         in_specs.append(pl.BlockSpec(memory_space=pl.ANY))
+        aliases = {len(args): 0}
         args.append(stacked)
-        aliases = {4: 0}
     return pl.pallas_call(
-        wgrad_kernel, grid=(m_dim // block_rows,), in_specs=in_specs,
+        kernel, grid=(m_dim // block_rows,), in_specs=in_specs,
         out_specs=pl.BlockSpec((1, block_rows, n_dim), lambda m: (layer_idx, m, 0)),
         out_shape=jax.ShapeDtypeStruct((n_layers, m_dim, n_dim), BF16),
         input_output_aliases=aliases,
-        cost_estimate=pl.CostEstimate(flops=4 * half * m_dim * n_dim, bytes_accessed=2 * (m_dim * n_dim + 2 * half * (m_dim + n_dim)), transcendentals=0),
+        scratch_shapes=[pltpu.VMEM((block_rows, depth), BF16)],
+        cost_estimate=pl.CostEstimate(flops=2 * depth * m_dim * n_dim, bytes_accessed=2 * (m_dim * n_dim + depth * (m_dim + n_dim)), transcendentals=0),
         compiler_params=pltpu.CompilerParams(vmem_limit_bytes=WG_VMEM),
     )(*args)
 
@@ -274,18 +338,24 @@
             return [qkv] + fused_mm(half, [(u_half, 0)] * 2, [w_gate, w_up], False, layer, 256, extras, epilogue, [(half, BF16, True)] * 2 + [(half, BF16, d_hid is not None)])
 
         def mlp_back(layer, n_rows, dy_half, gate_half, up_half):
-            return fused_mm(n_rows, [(dy_half, 0)], [w_down], True, layer, 256, [(gate_half, 0), (up_half, 0)], mlp_back_epilogue, [(n_rows, BF16)] * 3)
-
-        def wgrads(which, layer, u_halves, d_qkv, d_gate, d_up, o_halves, hidden, dy_halves, stacks):
-            lhs = {0: u_halves, 1: o_halves, 2: u_halves, 3: u_halves, 4: hidden}[which]
-            rhs = {0: d_qkv, 1: dy_halves, 2: d_gate, 3: d_up, 4: dy_halves}[which]
-            stacks[which] = wgrad(half, list(lhs), list(rhs), layer, n_layers, stacks[which], 256 if which == 1 else 512)
+            return fused_mm(n_rows, [(dy_half, 0)], [w_down], True, layer, 512, [(gate_half, 0), (up_half, 0)], mlp_back_epilogue, [(n_rows, BF16, True)] * 3)
+
+        def pieces(*arrays):
+            return [(arr, 0, arr.shape[0]) for arr in arrays]
+
+        def wgrads(which, layer, u_pieces, d_qkv, d_gate, d_up, o_halves, hidden, dy_halves, stacks):
+            lhs = {0: u_pieces, 1: pieces(*o_halves), 2: u_pieces, 3: u_pieces, 4: pieces(*hidden)}[which]
+            rhs = pieces(*{0: d_qkv, 1: dy_halves, 2: d_gate, 3: d_up, 4: dy_halves}[which])
+            stacks[which] = wgrad(lhs, rhs, layer, n_layers, stacks[which], 256 if which == 1 else 512)
 
         d_hid1 = dy_far = None
         for layer in range(n_layers):
             last = layer == n_layers - 1
             x_f32 = x_cur.astype(F32)
-            u_loc = rms_scale(x_f32, norm_gain[layer]).astype(BF16)
+            if layer == 0:
+                u_loc, dy_vmem = norm(x_cur, norm_gain, layer, dy_loc)
+            else:
+                u_loc = rms_scale(x_f32, norm_gain[layer]).astype(BF16)
             other = chip_swap(u_loc)
             u_near = jnp.concatenate([u_loc, core_swap(u_loc)], axis=0)
             near = project(layer, u_near, d_hid1[0] if last else None)
@@ -298,11 +368,11 @@
                 near[0], near[1], other = barrier(near[0], near[1], other)
             u_far = jnp.concatenate([other, core_swap(other)], axis=0)
             if layer == 0:
-                dy_start, u_far = barrier(dy_loc, u_far)
+                dy_start, u_far = barrier(dy_vmem, u_far)
                 dy_other = chip_swap(dy_start)
             far = project(layer, u_far, d_hid1[1] if last else None)
             rot_qkv, o_n, o_f, lse = attn_fwd(base, near[0], far[0], cos_tab, sin_tab)
-            saved.append({'x': x_cur, 'u': u_loc, 'rot': rot_qkv, 'o': ((o_n, 0), (o_f, 0)), 'lse': lse, 'gate': (near[1], far[1]), 'up': (near[2], far[2])})
+            saved.append({'x': x_cur, 'u': u_loc, 'rot': rot_qkv, 'o': (o_n, o_f), 'lse': lse, 'gate': (near[1], far[1]), 'up': (near[2], far[2])})
             if last:
                 break
             split_outs = [(rows, F32)] * 2
@@ -333,7 +403,7 @@
             x_sum = x_f32 + (near_keep + near_recv)
             x_sum, d_hid1[0], d_hid1[1], d_attn1_f, far_a, far_b = barrier(x_sum, d_hid1[0], d_hid1[1], d_attn1_f, far_a, far_b)
             x_cur = (x_sum + jnp.concatenate([far_a, far_b], axis=1)).astype(BF16)
-        u_halves = ((u_near, 0), (u_far, 0))
+        u_pieces = pieces(u_near, u_far)
         grad_cur = dy_loc
         stacks = [None] * 5
         gain_grads = [None] * n_layers
@@ -341,7 +411,7 @@
             kept = saved[layer]
             (gate_n, gate_f), (up_n, up_f) = kept['gate'], kept['up']
             if layer == n_layers - 1:
-                dy_halves = ((dy_near, 0), (dy_far, 0))
+                dy_halves = (dy_near, dy_far)
                 d_attn = ((d_attn1_n, 0), (d_attn1_f, 0))
             else:
                 dy_near = jnp.concatenate([grad_cur, core_swap(grad_cur)], axis=0)
@@ -353,22 +423,22 @@
                 back_n = mlp_back(layer, half, dy_near, gate_n, up_n)
                 stacks[4], back_n[0], dy_other = barrier(stacks[4], back_n[0], dy_other)
                 dy_far = jnp.concatenate([dy_other, core_swap(dy_other)], axis=0)
-                dy_halves = ((dy_near, 0), (dy_far, 0))
+                dy_halves = (dy_near, dy_far)
                 d_attn_far = dot_t(dy_far, w_out[layer]).astype(BF16)
                 d_attn = ((d_attn_near, 0), (d_attn_far, 0))
                 back_f = mlp_back(layer, half, dy_far, gate_f, up_f)
                 u_start, stacks[0], stacks[2], stacks[3], dy_other = barrier(kept['u'], stacks[0], stacks[2], stacks[3], dy_other)
                 u_other = chip_swap(u_start)
-                u_near = jnp.concatenate([u_start, core_swap(u_start)], axis=0)
-                u_far = jnp.concatenate([u_other, core_swap(u_other)], axis=0)
-                u_halves = ((u_near, 0), (u_far, 0))
-            hidden, d_gate, d_up = [((back_n[idx], 0), (back_f[idx], 0)) for idx in range(3)]
+                u_pieces = pieces(u_start, core_swap(u_start), u_other, core_swap(u_other))
+            hidden, d_gate, d_up = [(back_n[idx], back_f[idx]) for idx in range(3)]
             qkv_n, qkv_f = attn_bwd(base, kept['rot'], kept['lse'], d_attn, cos_tab, sin_tab)
-            d_qkv = ((qkv_n, 0), (qkv_f, 0))
-            w_args = (layer, u_halves, d_qkv, d_gate, d_up, kept['o'], hidden, dy_halves, stacks)
+            d_qkv = (qkv_n, qkv_f)
+            w_args = (layer, u_pieces, d_qkv, d_gate, d_up, kept['o'], hidden, dy_halves, stacks)
+
+            w_args = (layer, u_pieces, d_qkv, d_gate, d_up, kept['o'], hidden, dy_halves, stacks)
 
             def dgrad(side):
-                return fused_mm(half, [d_qkv[side], d_gate[side], d_up[side]], [w_qkv, w_gate, w_up], True, layer, 512, [], split_sum_epilogue, [(rows, F32)] * 2)
+                return fused_mm(half, [(d_qkv[side], 0), (d_gate[side], 0), (d_up[side], 0)], [w_qkv, w_gate, w_up], True, layer, 512, [], split_sum_epilogue, [(rows, F32)] * 2)
 
             far_keep, far_send = dgrad(1)
             far_recv = core_swap(far_send)
@@ -376,11 +446,12 @@
             stacks[1], far_recv = barrier(stacks[1], far_recv)
             far_sum = far_keep + far_recv
             from_far = chip_swap(far_sum)
-            qkv_n, far_sum = barrier(qkv_n, far_sum)
-            d_qkv = ((qkv_n, 0), (qkv_f, 0))
+            qkv_n, hid_n, gate_n, up_n, far_sum = barrier(qkv_n, hidden[0], d_gate[0], d_up[0], far_sum)
+            hidden, d_gate, d_up = (hid_n, hidden[1]), (gate_n, d_gate[1]), (up_n, d_up[1])
+            d_qkv = (qkv_n, qkv_f)
             near_keep, near_send = dgrad(0)
             near_recv = core_swap(near_send)
-            w_args = (layer, u_halves, d_qkv, d_gate, d_up, kept['o'], hidden, dy_halves, stacks)
+            w_args = (layer, u_pieces, d_qkv, d_gate, d_up, kept['o'], hidden, dy_halves, stacks)
             wgrads(0, *w_args)
             wgrads(2, *w_args)
             wgrads(3, *w_args)
@@ -393,14 +464,11 @@
             d_x_norm, gain_grads[layer] = norm_pull(d_normed.astype(F32))
             grad_cur = (grad_cur.astype(F32) + d_x_norm).astype(BF16)
             if layer != 0:
-                dy_halves = tuple(dy_halves)
-                hid_n, hid_f, grad_tie = barrier(back_n[0], back_f[0], grad_cur)
-                grad_cur = grad_tie
-                w_args = (layer, u_halves, d_qkv, d_gate, d_up, kept['o'], ((hid_n, 0), (hid_f, 0)), dy_halves, stacks)
+                hid_n, hid_f, grad_cur = barrier(hidden[0], hidden[1], grad_cur)
+                w_args = (layer, u_pieces, d_qkv, d_gate, d_up, kept['o'], (hid_n, hid_f), dy_halves, stacks)
                 wgrads(4, *w_args)
         gain = jnp.stack(gain_grads)
-        gain = gain + core_swap(gain)
-        gain = gain + chip_swap(gain)
+        gain = (gain + core_swap(gain)) + (chip_swap(gain) + lax.ppermute(gain, 'tp', CROSS_PAIRS))
         return (grad_cur, gain, stacks[0], stacks[1], stacks[2], stacks[3], stacks[4])
 
     return jax.shard_map(device_program, mesh=mesh, in_specs=(row_spec, row_spec, P(None, None), col_spec, inner_spec, col_spec, col_spec, inner_spec), out_specs=(row_spec, P('dp', None), P('dp', None, 'tp'), P('dp', 'tp', None), P('dp', None, 'tp'), P('dp', None, 'tp'), P('dp', 'tp', None)), check_vma=False)

time: 638 us -> 667 us (1.045)
  waiting for transfers between devices: 84.7 us -> 118 us
    ppermute x10, waiting for transfers between devices: 77.1 us -> 111 us  [chip_swap(): return lax.ppermute(values, 'tp', CHIP_PAIRS)]
    unnamed x159 -> x150, local copies, waits for them, and re-layouts: 15.6 us -> 14.2 us
    pallas_call x10 -> x11, Pallas kernels: 133 us -> 135 us  [the longest x10 132 us: wgrad(): pl.pallas_call(kernel, grid=(m_dim // block_rows,), in_specs=in_specs, ou...]
  transfers between devices with their start and end apart: 28 -> 29, of which waited for: 13 -> 13; matrix products, arithmetic and copies ran while one was open for 11% -> 9% of each run, Pallas kernels for 47% -> 37%
where the time goes in v1:
time: 667 us; the launch traced here: 658 us
  Pallas kernels  412 us (62%)
  waiting for transfers between devices  118 us (18%)
  matrix products  60.1 us (9%)
  other arithmetic  29.7 us (4%)
  starting transfers between devices  19.8 us (3%)
  local copies, waits for them, and re-layouts  15.4 us (2%)
    pallas_call x13, Pallas kernels, fused_mm(): pl.pallas_call(kernel, grid=(steps,), in_specs=in_specs, out_specs=[pl.Bl...  216 us
    pallas_call x10, Pallas kernels, wgrad(): pl.pallas_call(kernel, grid=(m_dim // block_rows,), in_specs=in_specs, ou...  132 us
    ppermute x10, waiting for transfers between devices, chip_swap(): return lax.ppermute(values, 'tp', CHIP_PAIRS)  111 us
    pallas_call x2, Pallas kernels, attn_bwd(): pl.pallas_call(attn_bwd_kernel, grid=(groups,), name='attn_bwd', in_specs...  33.6 us
    dot_general x6, matrix products, dot_t(): lax.dot_general(lhs, rhs, (((1,), (1,)), ((), ())), preferred_element_typ...  32.5 us
    pallas_call x2, Pallas kernels, attn_fwd(): pl.pallas_call(attn_fwd_kernel, grid=(groups,), name='attn_fwd', in_specs...  28.1 us
    dot_general x4, matrix products, dot(): return jnp.dot(lhs, rhs, preferred_element_type=F32)  27.6 us
    ppermute x10, starting transfers between devices, chip_swap(): return lax.ppermute(values, 'tp', CHIP_PAIRS)  16.9 us
  transfers between devices with their start and end apart: 29, of which 13 were waited for; matrix products, arithmetic and copies ran while one was open for 9% of the time, Pallas kernels for 37%

profile of v1, /device:TPU:0, one launch (start us, length us, event | category | flops | bytes accessed | tf_op | source)
XLA Modules:
  0.0 657.8 jit_solution(15342927067900207365)
XLA Ops:
  2.8 2.6 norm.1
  6.3 3.0 collective-permute-start.2
  11.1 6.8 %fusion.51.qn_ref = bf16[512,1280]{1,0:T(8,128)(2,1)S(1)} fusion(bf16[512,3072]{1,0:T(8,128)(2,1)S(1)} %constant_dynamic-update-slice_fusion.refs_0_.refs_1_, bf16[2,3072,1280]{2,1,0:T(8,128)(2,1)} %refs_3_.21), kind=kOutput, calls=%fused_computation.67 | convolution fusion | flops 4027187200 | bytes 12320768 | tf_op jit(solution)/shard_map/dot_general | solution.py:56
  18.1 3.5 fusion.63.dn_ref
  21.6 18.5 %shard_map.135 = (bf16[512,2048]{1,0:T(8,128)(2,1)}, bf16[512,2048]{1,0:T(8,128)(2,1)}, bf16[512,2048]{1,0:T(8,128)(2,1)S(1)}) custom-call(bf16[512,3072]{1,0:T(8,128)(2,1)S(1)} %constant_dynamic-update-slice_fusion.refs_0_.refs_1_, bf16[512,3072]{1,0:T(8,128)(2,1)S(1)} %constant_dynamic-update-slice_fusion.refs_0_.refs_1_, bf16[2,3072,2048]{2,1,0:T(8,128)(2,1)} %refs_4_.7, ...), custom_call_target="tpu_custom_call" | custom-call | flops 12884901888 | bytes 35651584 | tf_op jit(solution)/shard_map/pallas_call | solution.py:286
  40.1 3.9 collective-permute-done.2
  44.0 2.0 fusion.77
  47.7 2.1 pad_maximum_fusion.refs_0_.refs_1_
  49.8 6.7 %fusion.54.qf_ref = bf16[512,1280]{1,0:T(8,128)(2,1)S(1)} fusion(bf16[512,3072]{1,0:T(8,128)(2,1)S(1)} %pad_maximum_fusion.refs_0_.refs_1_, bf16[2,3072,1280]{2,1,0:T(8,128)(2,1)} %refs_3_.21), kind=kOutput, calls=%fused_computation.68 | convolution fusion | flops 4027187200 | bytes 12320768 | tf_op jit(solution)/shard_map/dot_general | solution.py:56
  56.5 18.3 %shard_map.136 = (bf16[512,2048]{1,0:T(8,128)(2,1)}, bf16[512,2048]{1,0:T(8,128)(2,1)}, bf16[512,2048]{1,0:T(8,128)(2,1)S(1)}) custom-call(bf16[512,3072]{1,0:T(8,128)(2,1)S(1)} %pad_maximum_fusion.refs_0_.refs_1_, bf16[512,3072]{1,0:T(8,128)(2,1)S(1)} %pad_maximum_fusion.refs_0_.refs_1_, bf16[2,3072,2048]{2,1,0:T(8,128)(2,1)} %refs_4_.7, ...), custom_call_target="tpu_custom_call" | custom-call | flops 12884901888 | bytes 35651584 | tf_op jit(solution)/shard_map/pallas_call | solution.py:286
  74.9 14.2 %attn_fwd.2 = (bf16[1024,1280]{1,0:T(8,128)(2,1)}, bf16[512,768]{1,0:T(8,128)(2,1)S(1)}, bf16[512,768]{1,0:T(8,128)(2,1)S(1)}, f32[2,8,1024]{2,1,0:T(8,128)S(1)}) custom-call(s32[4]{0:T(128)S(1)} %iota_xor_fusion.base_ref, bf16[512,1280]{1,0:T(8,128)(2,1)S(1)} %fusion.51.qn_ref, bf16[512,1280]{1,0:T(8,128)(2,1)S(1)} %fusion.54.qf_ref, ...), custom_call_target="tpu_custom_call" | custom-call | flops 8000000000 | bytes 8000000 | tf_op jit(solution)/shard_map/attn_fwd/pallas_call | solution.py:127
  89.1 7.3 %shard_map.137 = (f32[256,1536]{1,0:T(8,128)S(1)}, f32[256,1536]{1,0:T(8,128)S(1)}) custom-call(bf16[512,768]{1,0:T(8,128)(2,1)S(1)} %get-tuple-element.118.refs_0_.refs_1_, bf16[512,2048]{1,0:T(8,128)(2,1)S(1)} %get-tuple-element.116.refs_1_, bf16[2,768,3072]{2,1,0:T(8,128)(2,1)S(1)} %bitcast.61, bf16[2,2048,3072]{2,1,0:T(8,128)(2,1)} %refs_1_.3), custom_call_target="tpu_custom_call" | custom-call | flops 4429185024 | bytes 14680064 | tf_op jit(solution)/shard_map/pallas_call | solution.py:286
  96.6 7.0 %shard_map.138 = (f32[256,1536]{1,0:T(8,128)S(1)}, f32[256,1536]{1,0:T(8,128)S(1)}) custom-call(bf16[512,768]{1,0:T(8,128)(2,1)S(1)} %get-tuple-element.118.refs_0_.refs_1_, bf16[512,2048]{1,0:T(8,128)(2,1)S(1)} %get-tuple-element.116.refs_1_, bf16[2,768,3072]{2,1,0:T(8,128)(2,1)S(1)} %bitcast.61, bf16[2,2048,3072]{2,1,0:T(8,128)(2,1)} %refs_1_.3), custom_call_target="tpu_custom_call" | custom-call | flops 4429185024 | bytes 14680064 | tf_op jit(solution)/shard_map/pallas_call | solution.py:286
  103.9 1.7 collective-permute-start.7
  107.9 12.8 %shard_map.139 = (f32[256,3072]{1,0:T(8,128)S(1)}, f32[256,3072]{1,0:T(8,128)}) custom-call(bf16[512,768]{1,0:T(8,128)(2,1)S(1)} %get-tuple-element.125.refs_0_, bf16[512,2048]{1,0:T(8,128)(2,1)S(1)} %get-tuple-element.126.refs_1_, bf16[2,768,3072]{2,1,0:T(8,128)(2,1)S(1)} %bitcast.61, bf16[2,2048,3072]{2,1,0:T(8,128)(2,1)} %refs_1_.3), custom_call_target="tpu_custom_call" | custom-call | flops 8858370048 | bytes 26476544 | tf_op jit(solution)/shard_map/pallas_call | solution.py:286
  122.0 1.7 collective-permute-start.10
  123.8 17.5 %collective-permute-done.7 = bf16[256,3072]{1,0:T(8,128)(2,1)} collective-permute-done((bf16[256,3072]{1,0:T(8,128)(2,1)S(1)}, bf16[256,3072]{1,0:T(8,128)(2,1)}, u32[]{:S(2)}, u32[]{:S(2)}) %collective-permute-start.7) | collective-permute-done | bytes 1572896 | tf_op jit(solution)/shard_map/ppermute | solution.py:31
  141.3 10.1 %fusion.45.refs_4_ = bf16[512,2048]{1,0:T(8,128)(2,1)S(1)} fusion(bf16[512,3072]{1,0:T(8,128)(2,1)S(1)} %copy-done.30, bf16[2,2048,3072]{2,1,0:T(8,128)(2,1)} %refs_1_.3), kind=kOutput, calls=%fused_computation.65 | convolution fusion | flops 6443499520 | bytes 17825792 | tf_op jit(solution)/shard_map/dot_general | solution.py:60
  153.0 10.8 %fusion.48.refs_4_ = bf16[512,2048]{1,0:T(8,128)(2,1)S(1)} fusion(bf16[512,3072]{1,0:T(8,128)(2,1)S(1)} %constant_dynamic-update-slice_fusion.4.refs_3_, bf16[2,2048,3072]{2,1,0:T(8,128)(2,1)} %refs_1_.3), kind=kOutput, calls=%fused_computation.66 | convolution fusion | flops 6443499520 | bytes 17825792 | tf_op jit(solution)/shard_map/dot_general | solution.py:60
  163.9 2.6 fusion.66.df_ref
  166.6 1.8 convert_add_fusion
  168.3 6.6 %collective-permute-done.9 = f32[256,1536]{1,0:T(8,128)} collective-permute-done((f32[256,1536]{1,0:T(8,128)}, f32[256,1536]{1,0:T(8,128)}, u32[]{:S(2)}, u32[]{:S(2)}) %collective-permute-start.9) | collective-permute-done | bytes 1572896 | tf_op jit(solution)/shard_map/ppermute | solution.py:31
  175.0 33.0 %collective-permute-done.10 = f32[256,1536]{1,0:T(8,128)} collective-permute-done((f32[256,1536]{1,0:T(8,128)}, f32[256,1536]{1,0:T(8,128)}, u32[]{:S(2)}, u32[]{:S(2)}) %collective-permute-start.10) | collective-permute-done | bytes 1572896 | tf_op jit(solution)/shard_map/ppermute | solution.py:31
  207.9 2.4 fusion.40
  211.0 1.8 collective-permute-start.12
  214.4 7.4 %fusion.57.qn_ref = bf16[512,1280]{1,0:T(8,128)(2,1)S(1)} fusion(bf16[2,3072,1280]{2,1,0:T(8,128)(2,1)} %refs_3_.21, bf16[256,3072]{1,0:T(8,128)(2,1)S(1)} %collective-permute-done.11, bf16[256,3072]{1,0:T(8,128)(2,1)S(1)} %fusion.33), kind=kOutput, calls=%fused_computation.69 | convolution fusion | flops 4033478656 | bytes 12320768 | tf_op jit(solution)/shard_map/dot_general | solution.py:56
  222.1 19.6 %shard_map.140 = (bf16[512,2048]{1,0:T(8,128)(2,1)}, bf16[512,2048]{1,0:T(8,128)(2,1)}, bf16[512,2048]{1,0:T(8,128)(2,1)}) custom-call(bf16[512,3072]{1,0:T(8,128)(2,1)S(1)} %pad_maximum_fusion.1.refs_0_.refs_1_, bf16[512,3072]{1,0:T(8,128)(2,1)S(1)} %pad_maximum_fusion.1.refs_0_.refs_1_, bf16[2,3072,2048]{2,1,0:T(8,128)(2,1)} %refs_4_.7, ...), custom_call_target="tpu_custom_call" | custom-call | flops 12884901888 | bytes 35651584 | tf_op jit(solution)/shard_map/pallas_call | solution.py:286
  241.7 6.1 collective-permute-done.12
  247.9 3.3 collective-permute-done.13
  251.3 6.7 %fusion.60.qf_ref = bf16[512,1280]{1,0:T(8,128)(2,1)S(1)} fusion(bf16[512,3072]{1,0:T(8,128)(2,1)S(1)} %constant_dynamic-update-slice_fusion.6.refs_0_.refs_1_, bf16[2,3072,1280]{2,1,0:T(8,128)(2,1)} %refs_3_.21), kind=kOutput, calls=%fused_computation.70 | convolution fusion | flops 4027187200 | bytes 12320768 | tf_op jit(solution)/shard_map/dot_general | solution.py:56
  258.0 19.5 %shard_map.141 = (bf16[512,2048]{1,0:T(8,128)(2,1)}, bf16[512,2048]{1,0:T(8,128)(2,1)}, bf16[512,2048]{1,0:T(8,128)(2,1)}) custom-call(bf16[512,3072]{1,0:T(8,128)(2,1)S(1)} %constant_dynamic-update-slice_fusion.6.refs_0_.refs_1_, bf16[512,3072]{1,0:T(8,128)(2,1)S(1)} %constant_dynamic-update-slice_fusion.6.refs_0_.refs_1_, bf16[2,3072,2048]{2,1,0:T(8,128)(2,1)} %refs_4_.7, ...), custom_call_target="tpu_custom_call" | custom-call | flops 12884901888 | bytes 35651584 | tf_op jit(solution)/shard_map/pallas_call | solution.py:286
  277.5 13.9 %attn_fwd.3 = (bf16[1024,1280]{1,0:T(8,128)(2,1)}, bf16[512,768]{1,0:T(8,128)(2,1)S(1)}, bf16[512,768]{1,0:T(8,128)(2,1)S(1)}, f32[2,8,1024]{2,1,0:T(8,128)S(1)}) custom-call(s32[4]{0:T(128)S(1)} %iota_xor_fusion.base_ref, bf16[512,1280]{1,0:T(8,128)(2,1)S(1)} %fusion.57.qn_ref, bf16[512,1280]{1,0:T(8,128)(2,1)S(1)} %fusion.60.qf_ref, ...), custom_call_target="tpu_custom_call" | custom-call | flops 8000000000 | bytes 8000000 | tf_op jit(solution)/shard_map/attn_fwd/pallas_call | solution.py:127
  293.2 16.8 %attn_bwd.2 = (bf16[512,1280]{1,0:T(8,128)(2,1)S(1)}, bf16[512,1280]{1,0:T(8,128)(2,1)S(1)}) custom-call(s32[4]{0:T(128)S(1)} %iota_xor_fusion.base_ref, bf16[1024,1280]{1,0:T(8,128)(2,1)S(1)} %copy-done.49, f32[2,8,1024]{2,1,0:T(8,128)S(1)} %get-tuple-element.143.lse_ref, bf16[512,768]{1,0:T(8,128)(2,1)S(1)} %copy-done.47, ...), custom_call_target="tpu_custom_call" | custom-call | flops 20000000000 | bytes 8000000 | tf_op jit(solution)/shard_map/attn_bwd/pallas_call | solution.py:184
  310.0 22.4 %shard_map.142 = (f32[256,3072]{1,0:T(8,128)S(1)}, f32[256,3072]{1,0:T(8,128)}) custom-call(bf16[512,1280]{1,0:T(8,128)(2,1)S(1)} %get-tuple-element.150.refs_0_.refs_3_, bf16[512,2048]{1,0:T(8,128)(2,1)S(1)} %copy-done.24, bf16[512,2048]{1,0:T(8,128)(2,1)S(1)} %copy-done.23, bf16[2,3072,1280]{2,1,0:T(8,128)(2,1)} %refs_3_.21, ...), custom_call_target="tpu_custom_call" | custom-call | flops 16911433728 | bytes 44826624 | tf_op jit(solution)/shard_map/pallas_call | solution.py:286
  332.6 1.9 copy-done.31
  334.5 7.2 %shard_map.143.refs_4_ = bf16[2,768,3072]{2,1,0:T(8,128)(2,1)} custom-call(bf16[512,768]{1,0:T(8,128)(2,1)S(1)} %get-tuple-element.155.refs_0_, bf16[512,768]{1,0:T(8,128)(2,1)S(1)} %get-tuple-element.156.refs_1_, bf16[512,3072]{1,0:T(8,128)(2,1)S(1)} %copy-done.31, bf16[512,3072]{1,0:T(8,128)(2,1)S(1)} %copy-done.34), custom_call_target="tpu_custom_call" | custom-call | flops 4831838208 | bytes 12582912 | tf_op jit(solution)/shard_map/pallas_call | solution.py:253
  341.7 2.2 add.75
  345.6 21.4 %shard_map.144 = (f32[256,3072]{1,0:T(8,128)S(1)}, f32[256,3072]{1,0:T(8,128)S(1)}) custom-call(bf16[512,1280]{1,0:T(8,128)(2,1)S(1)} %get-tuple-element.161.refs_0_.refs_2_, bf16[512,2048]{1,0:T(8,128)(2,1)S(1)} %copy-done.22, bf16[512,2048]{1,0:T(8,128)(2,1)S(1)} %copy-done.21, bf16[2,3072,1280]{2,1,0:T(8,128)(2,1)} %refs_3_.21, ...), custom_call_target="tpu_custom_call" | custom-call | flops 16911433728 | bytes 44826624 | tf_op jit(solution)/shard_map/pallas_call | solution.py:286
  367.1 10.9 %shard_map.145.refs_6_ = bf16[2,3072,1280]{2,1,0:T(8,128)(2,1)} custom-call(bf16[512,3072]{1,0:T(8,128)(2,1)S(1)} %pad_maximum_fusion.1.refs_0_.refs_1_, bf16[512,3072]{1,0:T(8,128)(2,1)S(1)} %constant_dynamic-update-slice_fusion.6.refs_0_.refs_1_, bf16[512,1280]{1,0:T(8,128)(2,1)S(1)} %get-tuple-element.161.refs_0_.refs_2_, bf16[512,1280]{1,0:T(8,128)(2,1)S(1)} %copy-done.28), custom_call_target="tpu_custom_call" | custom-call | flops 8053063680 | bytes 16777216 | tf_op jit(solution)/shard_map/pallas_call | solution.py:253
  377.9 16.0 %shard_map.146.refs_6_ = bf16[2,3072,2048]{2,1,0:T(8,128)(2,1)} custom-call(bf16[512,3072]{1,0:T(8,128)(2,1)S(1)} %pad_maximum_fusion.1.refs_0_.refs_1_, bf16[512,3072]{1,0:T(8,128)(2,1)S(1)} %constant_dynamic-update-slice_fusion.6.refs_0_.refs_1_, bf16[512,2048]{1,0:T(8,128)(2,1)S(1)} %copy-done.22, bf16[512,2048]{1,0:T(8,128)(2,1)S(1)} %copy-done.24), custom_call_target="tpu_custom_call" | custom-call | flops 12884901888 | bytes 23068672 | tf_op jit(solution)/shard_map/pallas_call | solution.py:253
  393.9 16.0 %shard_map.147.refs_6_ = bf16[2,3072,2048]{2,1,0:T(8,128)(2,1)} custom-call(bf16[512,3072]{1,0:T(8,128)(2,1)S(1)} %pad_maximum_fusion.1.refs_0_.refs_1_, bf16[512,3072]{1,0:T(8,128)(2,1)S(1)} %constant_dynamic-update-slice_fusion.6.refs_0_.refs_1_, bf16[512,2048]{1,0:T(8,128)(2,1)S(1)} %copy-done.21, bf16[512,2048]{1,0:T(8,128)(2,1)S(1)} %copy-done.23), custom_call_target="tpu_custom_call" | custom-call | flops 12884901888 | bytes 23068672 | tf_op jit(solution)/shard_map/pallas_call | solution.py:253
  409.9 4.4 collective-permute-done.16
  414.4 4.2 fusion.34
  418.6 2.7 fusion.37
  421.4 1.8 collective-permute-start.18
  423.2 16.0 %shard_map.148.refs_4_ = bf16[2,2048,3072]{2,1,0:T(8,128)(2,1)} custom-call(bf16[512,2048]{1,0:T(8,128)(2,1)S(1)} %copy-done.43, bf16[512,2048]{1,0:T(8,128)(2,1)S(1)} %copy-done.44, bf16[512,3072]{1,0:T(8,128)(2,1)S(1)} %copy-done.32, bf16[512,3072]{1,0:T(8,128)(2,1)S(1)} %copy-done.35), custom_call_target="tpu_custom_call" | custom-call | flops 12884901888 | bytes 23068672 | tf_op jit(solution)/shard_map/pallas_call | solution.py:253
  440.8 12.8 %shard_map.149 = (bf16[512,2048]{1,0:T(8,128)(2,1)}, bf16[512,2048]{1,0:T(8,128)(2,1)}, bf16[512,2048]{1,0:T(8,128)(2,1)}) custom-call(bf16[512,3072]{1,0:T(8,128)(2,1)S(1)} %constant_dynamic-update-slice_fusion.8.refs_0_.refs_2_, bf16[2,2048,3072]{2,1,0:T(8,128)(2,1)} %refs_1_.3, bf16[512,2048]{1,0:T(8,128)(2,1)S(1)} %copy-done.17, ...), custom_call_target="tpu_custom_call" | custom-call | flops 6442450944 | bytes 19922944 | tf_op jit(solution)/shard_map/pallas_call | solution.py:286
  453.6 4.6 collective-permute-done.18
  458.4 2.7 fusion.69.dn_ref
  461.7 2.7 fusion.72.df_ref
  464.5 12.7 %shard_map.150 = (bf16[512,2048]{1,0:T(8,128)(2,1)}, bf16[512,2048]{1,0:T(8,128)(2,1)}, bf16[512,2048]{1,0:T(8,128)(2,1)}) custom-call(bf16[512,3072]{1,0:T(8,128)(2,1)S(1)} %constant_dynamic-update-slice_fusion.10.refs_0_.refs_3_, bf16[2,2048,3072]{2,1,0:T(8,128)(2,1)} %refs_1_.3, bf16[512,2048]{1,0:T(8,128)(2,1)S(1)} %copy-done.19, ...), custom_call_target="tpu_custom_call" | custom-call | flops 6442450944 | bytes 19922944 | tf_op jit(solution)/shard_map/pallas_call | solution.py:286
  477.3 16.8 %attn_bwd.3 = (bf16[512,1280]{1,0:T(8,128)(2,1)S(1)}, bf16[512,1280]{1,0:T(8,128)(2,1)S(1)}) custom-call(s32[4]{0:T(128)S(1)} %iota_xor_fusion.base_ref, bf16[1024,1280]{1,0:T(8,128)(2,1)S(1)} %copy-done.48, f32[2,8,1024]{2,1,0:T(8,128)S(1)} %get-tuple-element.169.lse_ref, bf16[512,768]{1,0:T(8,128)(2,1)S(1)} %fusion.69.dn_ref, ...), custom_call_target="tpu_custom_call" | custom-call | flops 20000000000 | bytes 8000000 | tf_op jit(solution)/shard_map/attn_bwd/pallas_call | solution.py:184
  494.1 21.4 %shard_map.151 = (f32[256,3072]{1,0:T(8,128)S(1)}, f32[256,3072]{1,0:T(8,128)S(1)}) custom-call(bf16[512,1280]{1,0:T(8,128)(2,1)S(1)} %get-tuple-element.180.refs_0_.refs_5_, bf16[512,2048]{1,0:T(8,128)(2,1)S(1)} %copy-done.9, bf16[512,2048]{1,0:T(8,128)(2,1)S(1)} %copy-done.7, bf16[2,3072,1280]{2,1,0:T(8,128)(2,1)} %refs_3_.21, ...), custom_call_target="tpu_custom_call" | custom-call | flops 16911433728 | bytes 44826624 | tf_op jit(solution)/shard_map/pallas_call | solution.py:286
  517.6 34.8 %collective-permute-done.23.refs_2_ = bf16[256,3072]{1,0:T(8,128)(2,1)S(1)} collective-permute-done((bf16[256,3072]{1,0:T(8,128)(2,1)S(1)}, bf16[256,3072]{1,0:T(8,128)(2,1)S(1)}, u32[]{:S(2)}, u32[]{:S(2)}) %collective-permute-start.23) | collective-permute-done | bytes 1572896 | tf_op jit(solution)/shard_map/ppermute | solution.py:31
  552.4 7.0 %shard_map.152 = bf16[2,768,3072]{2,1,0:T(8,128)(2,1)} custom-call(bf16[512,768]{1,0:T(8,128)(2,1)S(1)} %copy-done.14, bf16[512,768]{1,0:T(8,128)(2,1)S(1)} %copy-done.12, bf16[512,3072]{1,0:T(8,128)(2,1)S(1)} %constant_dynamic-update-slice_fusion.8.refs_0_.refs_2_, ...), custom_call_target="tpu_custom_call", output_to_operand_aliasing={{}: (4, {})} | custom-call | flops 4831838208 | bytes 12582912 | tf_op jit(solution)/shard_map/pallas_call | solution.py:253
  559.5 2.2 add.79
  563.4 22.1 %shard_map.153 = (f32[256,3072]{1,0:T(8,128)S(1)}, f32[256,3072]{1,0:T(8,128)}) custom-call(bf16[512,1280]{1,0:T(8,128)(2,1)S(1)} %get-tuple-element.189.refs_0_.refs_4_, bf16[512,2048]{1,0:T(8,128)(2,1)S(1)} %copy-done.6, bf16[512,2048]{1,0:T(8,128)(2,1)S(1)} %copy-done.5, bf16[2,3072,1280]{2,1,0:T(8,128)(2,1)} %refs_3_.21, bf16[2,3072,2048]{2,1,0:T(8,128)(2,1)} %refs_4_.7, ...), custom_call_target="tpu_custom_call" | custom-call | flops 16911433728 | bytes 44826624 | tf_op jit(solution)/shard_map/pallas_call | solution.py:286
  585.5 1.8 copy-done.15
  589.0 15.8 %shard_map.157 = bf16[2,2048,3072]{2,1,0:T(8,128)(2,1)} custom-call(bf16[512,2048]{1,0:T(8,128)(2,1)S(1)} %copy-done.25, bf16[512,2048]{1,0:T(8,128)(2,1)S(1)} %copy-done.26, bf16[512,3072]{1,0:T(8,128)(2,1)S(1)} %constant_dynamic-update-slice_fusion.8.refs_0_.refs_2_, ...), custom_call_target="tpu_custom_call", output_to_operand_aliasing={{}: (4, {})} | custom-call | flops 12884901888 | bytes 23068672 | tf_op jit(solution)/shard_map/pallas_call | solution.py:253
  604.9 10.9 %shard_map.154 = bf16[2,3072,1280]{2,1,0:T(8,128)(2,1)} custom-call(bf16[256,3072]{1,0:T(8,128)(2,1)S(1)} %copy-done.4, bf16[256,3072]{1,0:T(8,128)(2,1)S(1)} %collective-permute-done.22.refs_1_, bf16[256,3072]{1,0:T(8,128)(2,1)S(1)} %collective-permute-done.23.refs_2_, ...), custom_call_target="tpu_custom_call", output_to_operand_aliasing={{}: (6, {})} | custom-call | flops 8053063680 | bytes 16777216 | tf_op jit(solution)/shard_map/pallas_call | solution.py:253
  615.8 16.0 %shard_map.155 = bf16[2,3072,2048]{2,1,0:T(8,128)(2,1)} custom-call(bf16[256,3072]{1,0:T(8,128)(2,1)S(1)} %copy-done.4, bf16[256,3072]{1,0:T(8,128)(2,1)S(1)} %collective-permute-done.22.refs_1_, bf16[256,3072]{1,0:T(8,128)(2,1)S(1)} %collective-permute-done.23.refs_2_, ...), custom_call_target="tpu_custom_call", output_to_operand_aliasing={{}: (6, {})} | custom-call | flops 12884901888 | bytes 23068672 | tf_op jit(solution)/shard_map/pallas_call | solution.py:253
  631.8 16.3 %shard_map.156 = bf16[2,3072,2048]{2,1,0:T(8,128)(2,1)} custom-call(bf16[256,3072]{1,0:T(8,128)(2,1)S(1)} %copy-done.4, bf16[256,3072]{1,0:T(8,128)(2,1)S(1)} %collective-permute-done.22.refs_1_, bf16[256,3072]{1,0:T(8,128)(2,1)S(1)} %collective-permute-done.23.refs_2_, ...), custom_call_target="tpu_custom_call", output_to_operand_aliasing={{}: (6, {})} | custom-call | flops 12884901888 | bytes 23068672 | tf_op jit(solution)/shard_map/pallas_call | solution.py:253
  648.2 3.5 fusion.35
  653.9 2.3 fusion.39
  (215 shorter events, 30.0 us)
Async XLA Ops:
  5.5 5.5 collective-permute-start
  6.3 11.6 %collective-permute-start.1 = (bf16[256,3072]{1,0:T(8,128)(2,1)}, bf16[256,3072]{1,0:T(8,128)(2,1)S(1)}, u32[]{:S(2)}, u32[]{:S(2)}) collective-permute-start(bf16[256,3072]{1,0:T(8,128)(2,1)} %dy_ref.1), channel_id=1, source_target_pairs={{0,1},{1,0},{2,3},{3,2},{4,5},{5,4},{6,7},{7,6}} | collective-permute-start | bytes 4718600 | tf_op jit(solution)/shard_map/ppermute | solution.py:27
  6.3 37.6 %collective-permute-start.2 = (bf16[256,3072]{1,0:T(8,128)(2,1)S(1)}, bf16[256,3072]{1,0:T(8,128)(2,1)}, u32[]{:S(2)}, u32[]{:S(2)}) collective-permute-start(bf16[256,3072]{1,0:T(8,128)(2,1)S(1)} %get-tuple-element.197.refs_0_), channel_id=1, source_target_pairs={{0,2},{2,0},{1,3},{3,1},{4,6},{6,4},{5,7},{7,5}} | collective-permute-start | bytes 4718600 | tf_op jit(solution)/shard_map/ppermute | solution.py:31
  44.0 3.8 collective-permute-start.3
  46.3 28.5 %copy-start.36 = (f32[1024,128]{1,0:T(8,128)}, f32[1024,128]{1,0:T(8,128)S(1)}, u32[]{:S(2)}) copy-start(f32[1024,128]{1,0:T(8,128)S(1)} %get-tuple-element.226.cos_ref) | copy-start | bytes 1572868
  46.3 28.5 %copy-start.38 = (f32[1024,128]{1,0:T(8,128)}, f32[1024,128]{1,0:T(8,128)S(1)}, u32[]{:S(2)}) copy-start(f32[1024,128]{1,0:T(8,128)S(1)} %get-tuple-element.227.sin_ref) | copy-start | bytes 1572868
  74.8 14.2 %slice-start.3 = ((s8[9437184]{0:T(1024)(128)(4,1)}), s8[4194304]{0:T(1024)(128)(4,1)S(1)}, s32[]{:S(2)}) async-start(s8[9437184]{0:T(1024)(128)(4,1)} %bitcast.60), calls=%async_computation.3 | async-start | bytes 8388608
  74.8 14.2 %slice-start.4 = ((s8[9437184]{0:T(1024)(128)(4,1)}), s8[4194304]{0:T(1024)(128)(4,1)S(1)}, s32[]{:S(2)}) async-start(s8[9437184]{0:T(1024)(128)(4,1)} %bitcast.60), calls=%async_computation.4 | async-start | bytes 8388608
  74.8 14.2 %slice-start.5 = ((s8[9437184]{0:T(1024)(128)(4,1)}), s8[1048576]{0:T(1024)(128)(4,1)S(1)}, s32[]{:S(2)}) async-start(s8[9437184]{0:T(1024)(128)(4,1)} %bitcast.60), calls=%async_computation.5 | async-start | bytes 2097152
  89.0 18.8 %copy-start.13 = (bf16[512,768]{1,0:T(8,128)(2,1)}, bf16[512,768]{1,0:T(8,128)(2,1)S(1)}, u32[]{:S(2)}) copy-start(bf16[512,768]{1,0:T(8,128)(2,1)S(1)} %get-tuple-element.125.refs_0_) | copy-start | bytes 2359300
  96.4 9.8 %collective-permute-start.5 = (f32[256,1536]{1,0:T(8,128)S(1)}, f32[256,1536]{1,0:T(8,128)S(1)}, u32[]{:S(2)}, u32[]{:S(2)}) collective-permute-start(f32[256,1536]{1,0:T(8,128)S(1)} %get-tuple-element.117), channel_id=1, source_target_pairs={{0,1},{1,0},{2,3},{3,2},{4,5},{5,4},{6,7},{7,6}} | collective-permute-start | bytes 4718600 | tf_op jit(solution)/shard_map/ppermute | solution.py:27
  103.6 17.1 %collective-permute-start.4 = (f32[256,1536]{1,0:T(8,128)S(1)}, f32[256,1536]{1,0:T(8,128)S(1)}, u32[]{:S(2)}, u32[]{:S(2)}) collective-permute-start(f32[256,1536]{1,0:T(8,128)S(1)} %get-tuple-element.119), channel_id=1, source_target_pairs={{0,1},{1,0},{2,3},{3,2},{4,5},{5,4},{6,7},{7,6}} | collective-permute-start | bytes 4718600 | tf_op jit(solution)/shard_map/ppermute | solution.py:27
  103.9 37.4 %collective-permute-start.7 = (bf16[256,3072]{1,0:T(8,128)(2,1)S(1)}, bf16[256,3072]{1,0:T(8,128)(2,1)}, u32[]{:S(2)}, u32[]{:S(2)}) collective-permute-start(bf16[256,3072]{1,0:T(8,128)(2,1)S(1)} %copy-done.46), channel_id=1, source_target_pairs={{0,2},{2,0},{1,3},{3,1},{4,6},{6,4},{5,7},{7,5}} | collective-permute-start | bytes 4718600 | tf_op jit(solution)/shard_map/ppermute | solution.py:31
  106.2 104.2 %copy-start.54 = (f32[1,3072]{1,0:T(1,128)}, f32[1,3072]{1,0:T(1,128)S(1)}, u32[]{:S(2)}) copy-start(f32[1,3072]{1,0:T(1,128)S(1)} %get-tuple-element.221) | copy-start | bytes 36868
  107.6 67.4 %collective-permute-start.9 = (f32[256,1536]{1,0:T(8,128)}, f32[256,1536]{1,0:T(8,128)}, u32[]{:S(2)}, u32[]{:S(2)}) collective-permute-start(f32[256,1536]{1,0:T(8,128)} %add.69), channel_id=1, source_target_pairs={{0,2},{2,0},{1,3},{3,1},{4,6},{6,4},{5,7},{7,5}} | collective-permute-start | bytes 4718600 | tf_op jit(solution)/shard_map/ppermute | solution.py:31
  120.7 20.6 %copy-start.30 = (bf16[512,3072]{1,0:T(8,128)(2,1)S(1)}, bf16[512,3072]{1,0:T(8,128)(2,1)}, u32[]{:S(2)}) copy-start(bf16[512,3072]{1,0:T(8,128)(2,1)} %copy-done.29) | copy-start | bytes 9437188
  120.7 45.9 %collective-permute-start.6 = (f32[256,3072]{1,0:T(8,128)}, f32[256,3072]{1,0:T(8,128)S(1)}, u32[]{:S(2)}, u32[]{:S(2)}) collective-permute-start(f32[256,3072]{1,0:T(8,128)} %get-tuple-element.129), channel_id=1, source_target_pairs={{0,1},{1,0},{2,3},{3,2},{4,5},{5,4},{6,7},{7,6}} | collective-permute-start | bytes 9437192 | tf_op jit(solution)/shard_map/ppermute | solution.py:27
  122.0 85.9 %collective-permute-start.10 = (f32[256,1536]{1,0:T(8,128)}, f32[256,1536]{1,0:T(8,128)}, u32[]{:S(2)}, u32[]{:S(2)}) collective-permute-start(f32[256,1536]{1,0:T(8,128)} %add.72), channel_id=1, source_target_pairs={{0,2},{2,0},{1,3},{3,1},{4,6},{6,4},{5,7},{7,5}} | collective-permute-start | bytes 4718600 | tf_op jit(solution)/shard_map/ppermute | solution.py:31
  141.3 11.6 %collective-permute-start.8 = (bf16[256,3072]{1,0:T(8,128)(2,1)}, bf16[256,3072]{1,0:T(8,128)(2,1)S(1)}, u32[]{:S(2)}, u32[]{:S(2)}) collective-permute-start(bf16[256,3072]{1,0:T(8,128)(2,1)} %collective-permute-done.7), channel_id=1, source_target_pairs={{0,1},{1,0},{2,3},{3,2},{4,5},{5,4},{6,7},{7,6}} | collective-permute-start | bytes 4718600 | tf_op jit(solution)/shard_map/ppermute | solution.py:27
  210.9 3.4 collective-permute-start.11
  211.0 36.8 %collective-permute-start.12 = (bf16[256,3072]{1,0:T(8,128)(2,1)S(1)}, bf16[256,3072]{1,0:T(8,128)(2,1)S(1)}, u32[]{:S(2)}, u32[]{:S(2)}) collective-permute-start(bf16[256,3072]{1,0:T(8,128)(2,1)S(1)} %fusion.33), channel_id=1, source_target_pairs={{0,2},{2,0},{1,3},{3,1},{4,6},{6,4},{5,7},{7,5}} | collective-permute-start | bytes 4718600 | tf_op jit(solution)/shard_map/ppermute | solution.py:31
  247.8 3.4 collective-permute-start.13
  258.0 19.6 %copy-start.37 = (f32[1024,128]{1,0:T(8,128)S(1)}, f32[1024,128]{1,0:T(8,128)}, u32[]{:S(2)}) copy-start(f32[1024,128]{1,0:T(8,128)} %copy-done.36) | copy-start | bytes 1572868
  258.0 19.5 %copy-start.39 = (f32[1024,128]{1,0:T(8,128)S(1)}, f32[1024,128]{1,0:T(8,128)}, u32[]{:S(2)}) copy-start(f32[1024,128]{1,0:T(8,128)} %copy-done.38) | copy-start | bytes 1572868
  277.5 14.0 %copy-start.47 = (bf16[512,768]{1,0:T(8,128)(2,1)S(1)}, bf16[512,768]{1,0:T(8,128)(2,1)}, u32[]{:S(2)}) copy-start(bf16[512,768]{1,0:T(8,128)(2,1)} %fusion.63.dn_ref) | copy-start | bytes 2359300
  293.2 16.8 %copy-start.23 = (bf16[512,2048]{1,0:T(8,128)(2,1)S(1)}, bf16[512,2048]{1,0:T(8,128)(2,1)}, u32[]{:S(2)}) copy-start(bf16[512,2048]{1,0:T(8,128)(2,1)} %get-tuple-element.153.refs_2_.refs_3_) | copy-start | bytes 6291460
  293.2 16.8 %copy-start.24 = (bf16[512,2048]{1,0:T(8,128)(2,1)S(1)}, bf16[512,2048]{1,0:T(8,128)(2,1)}, u32[]{:S(2)}) copy-start(bf16[512,2048]{1,0:T(8,128)(2,1)} %get-tuple-element.152.refs_1_.refs_3_) | copy-start | bytes 6291460
  310.0 22.4 %copy-start.27 = (bf16[512,1280]{1,0:T(8,128)(2,1)}, bf16[512,1280]{1,0:T(8,128)(2,1)S(1)}, u32[]{:S(2)}) copy-start(bf16[512,1280]{1,0:T(8,128)(2,1)S(1)} %get-tuple-element.150.refs_0_.refs_3_) | copy-start | bytes 3932164
  310.0 22.5 %copy-start.34 = (bf16[512,3072]{1,0:T(8,128)(2,1)S(1)}, bf16[512,3072]{1,0:T(8,128)(2,1)}, u32[]{:S(2)}) copy-start(bf16[512,3072]{1,0:T(8,128)(2,1)} %copy-done.33) | copy-start | bytes 9437188
  332.4 9.2 %collective-permute-start.14 = (f32[256,3072]{1,0:T(8,128)}, f32[256,3072]{1,0:T(8,128)S(1)}, u32[]{:S(2)}, u32[]{:S(2)}) collective-permute-start(f32[256,3072]{1,0:T(8,128)} %get-tuple-element.157), channel_id=1, source_target_pairs={{0,1},{1,0},{2,3},{3,2},{4,5},{5,4},{6,7},{7,6}} | collective-permute-start | bytes 9437192 | tf_op jit(solution)/shard_map/ppermute | solution.py:27
  343.8 70.6 %collective-permute-start.16 = (f32[256,3072]{1,0:T(8,128)}, f32[256,3072]{1,0:T(8,128)S(1)}, u32[]{:S(2)}, u32[]{:S(2)}) collective-permute-start(f32[256,3072]{1,0:T(8,128)} %add.75), channel_id=1, source_target_pairs={{0,2},{2,0},{1,3},{3,1},{4,6},{6,4},{5,7},{7,5}} | collective-permute-start | bytes 9437192 | tf_op jit(solution)/shard_map/ppermute | solution.py:31
  345.6 21.5 %copy-start.28 = (bf16[512,1280]{1,0:T(8,128)(2,1)S(1)}, bf16[512,1280]{1,0:T(8,128)(2,1)}, u32[]{:S(2)}) copy-start(bf16[512,1280]{1,0:T(8,128)(2,1)} %copy-done.27) | copy-start | bytes 3932164
  367.0 47.4 %collective-permute-start.15 = (f32[256,3072]{1,0:T(8,128)S(1)}, f32[256,3072]{1,0:T(8,128)}, u32[]{:S(2)}, u32[]{:S(2)}) collective-permute-start(f32[256,3072]{1,0:T(8,128)S(1)} %get-tuple-element.165), channel_id=1, source_target_pairs={{0,1},{1,0},{2,3},{3,2},{4,5},{5,4},{6,7},{7,6}} | collective-permute-start | bytes 9437192 | tf_op jit(solution)/shard_map/ppermute | solution.py:27
  393.9 20.5 %copy-start.51 = (bf16[256,3072]{1,0:T(8,128)(2,1)S(1)}, bf16[256,3072]{1,0:T(8,128)(2,1)}, u32[]{:S(2)}) copy-start(bf16[256,3072]{1,0:T(8,128)(2,1)} %copy-done.50) | copy-start | bytes 4718596
  393.9 20.5 %copy-start.55 = (f32[1,3072]{1,0:T(1,128)S(1)}, f32[1,3072]{1,0:T(1,128)}, u32[]{:S(2)}) copy-start(f32[1,3072]{1,0:T(1,128)} %copy-done.54) | copy-start | bytes 36868
  393.9 20.5 %copy-start.59 = (f32[256]{0:T(256)S(1)}, f32[256]{0:T(256)}, u32[]{:S(2)}) copy-start(f32[256]{0:T(256)} %copy-done.58) | copy-start | bytes 3076
  421.4 17.8 %copy-start.52 = (bf16[256,3072]{1,0:T(8,128)(2,1)}, bf16[256,3072]{1,0:T(8,128)(2,1)S(1)}, u32[]{:S(2)}) copy-start(bf16[256,3072]{1,0:T(8,128)(2,1)S(1)} %fusion.37) | copy-start | bytes 4718596
  421.4 17.9 %collective-permute-start.17 = (bf16[256,3072]{1,0:T(8,128)(2,1)S(1)}, bf16[256,3072]{1,0:T(8,128)(2,1)S(1)}, u32[]{:S(2)}, u32[]{:S(2)}) collective-permute-start(bf16[256,3072]{1,0:T(8,128)(2,1)S(1)} %fusion.37), channel_id=1, source_target_pairs={{0,1},{1,0},{2,3},{3,2},{4,5},{5,4},{6,7},{7,6}} | collective-permute-start | bytes 4718600 | tf_op jit(solution)/shard_map/ppermute | solution.py:27
  421.4 36.8 %collective-permute-start.18 = (bf16[256,3072]{1,0:T(8,128)(2,1)S(1)}, bf16[256,3072]{1,0:T(8,128)(2,1)S(1)}, u32[]{:S(2)}, u32[]{:S(2)}) collective-permute-start(bf16[256,3072]{1,0:T(8,128)(2,1)S(1)} %fusion.37), channel_id=1, source_target_pairs={{0,2},{2,0},{1,3},{3,1},{4,6},{6,4},{5,7},{7,5}} | collective-permute-start | bytes 4718600 | tf_op jit(solution)/shard_map/ppermute | solution.py:31
  423.2 16.3 %copy-start.18 = (bf16[512,2048]{1,0:T(8,128)(2,1)S(1)}, bf16[512,2048]{1,0:T(8,128)(2,1)}, u32[]{:S(2)}) copy-start(bf16[512,2048]{1,0:T(8,128)(2,1)} %get-tuple-element.173.refs_3_) | copy-start | bytes 6291460
  439.2 19.1 %slice-start.6 = ((s8[9437184]{0:T(1024)(128)(4,1)}), s8[4194304]{0:T(1024)(128)(4,1)S(1)}, s32[]{:S(2)}) async-start(s8[9437184]{0:T(1024)(128)(4,1)} %bitcast.62), calls=%async_computation.6 | async-start | bytes 8388608
  440.8 17.5 %slice-start.7 = ((s8[9437184]{0:T(1024)(128)(4,1)}), s8[4194304]{0:T(1024)(128)(4,1)S(1)}, s32[]{:S(2)}) async-start(s8[9437184]{0:T(1024)(128)(4,1)} %bitcast.62), calls=%async_computation.7 | async-start | bytes 8388608
  440.8 17.5 %slice-start.8 = ((s8[9437184]{0:T(1024)(128)(4,1)}), s8[1048576]{0:T(1024)(128)(4,1)S(1)}, s32[]{:S(2)}) async-start(s8[9437184]{0:T(1024)(128)(4,1)} %bitcast.62), calls=%async_computation.8 | async-start | bytes 2097152
  458.2 3.4 collective-permute-start.19
  477.2 16.8 %copy-start.7 = (bf16[512,2048]{1,0:T(8,128)(2,1)S(1)}, bf16[512,2048]{1,0:T(8,128)(2,1)}, u32[]{:S(2)}) copy-start(bf16[512,2048]{1,0:T(8,128)(2,1)} %get-tuple-element.184.refs_2_.refs_5_) | copy-start | bytes 6291460
  477.2 16.8 %copy-start.9 = (bf16[512,2048]{1,0:T(8,128)(2,1)S(1)}, bf16[512,2048]{1,0:T(8,128)(2,1)}, u32[]{:S(2)}) copy-start(bf16[512,2048]{1,0:T(8,128)(2,1)} %get-tuple-element.183.refs_1_.refs_5_) | copy-start | bytes 6291460
  494.1 21.7 %copy-start.4 = (bf16[256,3072]{1,0:T(8,128)(2,1)S(1)}, bf16[256,3072]{1,0:T(8,128)(2,1)}, u32[]{:S(2)}) copy-start(bf16[256,3072]{1,0:T(8,128)(2,1)} %copy-done.3) | copy-start | bytes 4718596
  494.1 23.4 %copy-start.60 = (f32[256]{0:T(256)S(1)}, f32[256]{0:T(256)}, u32[]{:S(2)}) copy-start(f32[256]{0:T(256)} %get-tuple-element.220) | copy-start | bytes 3076
  494.1 58.3 %copy-start.12 = (bf16[512,768]{1,0:T(8,128)(2,1)S(1)}, bf16[512,768]{1,0:T(8,128)(2,1)}, u32[]{:S(2)}) copy-start(bf16[512,768]{1,0:T(8,128)(2,1)} %copy-done.11) | copy-start | bytes 2359300
  494.1 58.3 %copy-start.14 = (bf16[512,768]{1,0:T(8,128)(2,1)S(1)}, bf16[512,768]{1,0:T(8,128)(2,1)}, u32[]{:S(2)}) copy-start(bf16[512,768]{1,0:T(8,128)(2,1)} %copy-done.13) | copy-start | bytes 2359300
  515.6 43.9 %collective-permute-start.20 = (f32[256,3072]{1,0:T(8,128)S(1)}, f32[256,3072]{1,0:T(8,128)S(1)}, u32[]{:S(2)}, u32[]{:S(2)}) collective-permute-start(f32[256,3072]{1,0:T(8,128)S(1)} %get-tuple-element.187), channel_id=1, source_target_pairs={{0,1},{1,0},{2,3},{3,2},{4,5},{5,4},{6,7},{7,6}} | collective-permute-start | bytes 9437192 | tf_op jit(solution)/shard_map/ppermute | solution.py:27
  515.7 36.7 %collective-permute-start.23 = (bf16[256,3072]{1,0:T(8,128)(2,1)S(1)}, bf16[256,3072]{1,0:T(8,128)(2,1)S(1)}, u32[]{:S(2)}, u32[]{:S(2)}) collective-permute-start(bf16[256,3072]{1,0:T(8,128)(2,1)S(1)} %copy-done.4), channel_id=1, source_target_pairs={{0,2},{2,0},{1,3},{3,1},{4,6},{6,4},{5,7},{7,5}} | collective-permute-start | bytes 4718600 | tf_op jit(solution)/shard_map/ppermute | solution.py:31
  517.5 87.4 %collective-permute-start.22 = (bf16[256,3072]{1,0:T(8,128)(2,1)S(1)}, bf16[256,3072]{1,0:T(8,128)(2,1)S(1)}, u32[]{:S(2)}, u32[]{:S(2)}) collective-permute-start(bf16[256,3072]{1,0:T(8,128)(2,1)S(1)} %copy-done.4), channel_id=1, source_target_pairs={{0,1},{1,0},{2,3},{3,2},{4,5},{5,4},{6,7},{7,6}} | collective-permute-start | bytes 4718600 | tf_op jit(solution)/shard_map/ppermute | solution.py:27
  552.4 52.5 %collective-permute-start.24 = (bf16[256,3072]{1,0:T(8,128)(2,1)S(1)}, bf16[256,3072]{1,0:T(8,128)(2,1)S(1)}, u32[]{:S(2)}, u32[]{:S(2)}) collective-permute-start(bf16[256,3072]{1,0:T(8,128)(2,1)S(1)} %collective-permute-done.23.refs_2_), channel_id=1, source_target_pairs={{0,1},{1,0},{2,3},{3,2},{4,5},{5,4},{6,7},{7,6}} | collective-permute-start | bytes 4718600 | tf_op jit(solution)/shard_map/ppermute | solution.py:27
  561.6 86.5 %collective-permute-start.25 = (f32[256,3072]{1,0:T(8,128)}, f32[256,3072]{1,0:T(8,128)S(1)}, u32[]{:S(2)}, u32[]{:S(2)}) collective-permute-start(f32[256,3072]{1,0:T(8,128)} %add.79), channel_id=1, source_target_pairs={{0,2},{2,0},{1,3},{3,1},{4,6},{6,4},{5,7},{7,5}} | collective-permute-start | bytes 9437192 | tf_op jit(solution)/shard_map/ppermute | solution.py:31
  563.4 24.1 %copy-start.26 = (bf16[512,2048]{1,0:T(8,128)(2,1)S(1)}, bf16[512,2048]{1,0:T(8,128)(2,1)}, u32[]{:S(2)}) copy-start(bf16[512,2048]{1,0:T(8,128)(2,1)} %get-tuple-element.202.refs_1_) | copy-start | bytes 6291460
  587.2 60.9 %collective-permute-start.21 = (f32[256,3072]{1,0:T(8,128)}, f32[256,3072]{1,0:T(8,128)}, u32[]{:S(2)}, u32[]{:S(2)}) collective-permute-start(f32[256,3072]{1,0:T(8,128)} %get-tuple-element.193), channel_id=1, source_target_pairs={{0,1},{1,0},{2,3},{3,2},{4,5},{5,4},{6,7},{7,6}} | collective-permute-start | bytes 9437192 | tf_op jit(solution)/shard_map/ppermute | solution.py:27
  615.8 16.0 %copy-start.8 = (bf16[512,2048]{1,0:T(8,128)(2,1)S(1)}, bf16[512,2048]{1,0:T(8,128)(2,1)}, u32[]{:S(2)}) copy-start(bf16[512,2048]{1,0:T(8,128)(2,1)} %get-tuple-element.184.refs_2_.refs_5_) | copy-start | bytes 6291460
  631.8 16.4 %copy-start.2 = (bf16[256,3072]{1,0:T(8,128)(2,1)S(1)}, bf16[256,3072]{1,0:T(8,128)(2,1)}, u32[]{:S(2)}) copy-start(bf16[256,3072]{1,0:T(8,128)(2,1)} %x_ref.1) | copy-start | bytes 4718596
  631.8 16.4 %copy-start.16 = (f32[256,3072]{1,0:T(8,128)S(1)}, f32[256,3072]{1,0:T(8,128)}, u32[]{:S(2)}) copy-start(f32[256,3072]{1,0:T(8,128)} %copy-done.15) | copy-start | bytes 9437188
  631.8 16.4 %copy-start.56 = (f32[1,3072]{1,0:T(1,128)S(1)}, f32[1,3072]{1,0:T(1,128)}, u32[]{:S(2)}) copy-start(f32[1,3072]{1,0:T(1,128)} %get-tuple-element.222) | copy-start | bytes 36868
  651.8 4.5 collective-permute-start.27
  653.2 3.4 collective-permute-start.28
  653.4 3.2 collective-permute-start.26
  (37 other events, 208.7 us)
